TPU v7x, 256 devices: a whole 4x4x8 slice. The times are simulated.
256 devices in a mesh: leaf: 16 (over z, core), grp: 16 (over y, x).
Axes of the slice: x: 4, y: 4, z: 8, core: 2. Of those that a mesh axis runs over, the one named last changes fastest.
Arguments:
- front_rows: bfloat16 [16384, 24576], P('leaf', 'grp'), may hold values from -0.0390625 to 0.0390625
- sample_matrix: bfloat16 [24576, 1024], P('grp'), may hold values from -6 to 6
- pivots: int32 [31, 512], replicated, may hold values from 0 to 1023, as said below
Outputs:
- bases: float32 [5, 16, 1024, 512], P(None, 'leaf', 'grp')
- top_sample: float32 [1024, 512], P('grp')
Inputs may be any that keep to these rules, and one draw needn't show every extreme that they name: `pivots`: row o_l + j (o_l = 2 * 16 - 2 * 16 / 2^l) holds node j of level l: 512 distinct column numbers of its 1024 columns; entries k * 32 to (k + 1) * 32 - 1 lie in k * 64 to (k + 1) * 64 - 1.
All inputs are finite; a program needn't handle non-finite values.
Results may differ from a plain program's by a relative error of at most 0.0003.
Values sent between devices are 32-bit elements; how exact they have to be, the bound alone decides.
A program may use at most 128 MiB of HBM per device.

v0:
```python
import jax
import jax.numpy as jnp
from jax import lax
from jax.sharding import PartitionSpec as P


def from_partner(x, axis, bit):
    return lax.ppermute(x, axis, [(i, i ^ 1 << bit) for i in range(lax.axis_size(axis))])


def contract_first(left_side, right_side):
    return lax.dot_general(
        left_side,
        right_side,
        (((0,), (0,)), ((), ())),
        precision=lax.Precision.HIGHEST,
        preferred_element_type=jnp.float32,
    )


def basis_from(gram, cross):
    factor = jnp.linalg.cholesky(gram)
    identity = jnp.eye(gram.shape[0], dtype=gram.dtype)
    inverse_factor = jax.scipy.linalg.solve_triangular(factor, identity, lower=True)
    gram_inverse = jnp.dot(
        inverse_factor.T,
        inverse_factor,
        precision=lax.Precision.HIGHEST,
        preferred_element_type=jnp.float32,
    )
    return jnp.dot(
        cross, gram_inverse, precision=lax.Precision.HIGHEST, preferred_element_type=jnp.float32
    )


def on_device(front_rows, sample_matrix, pivots):
    leaf_count = lax.axis_size("leaf")
    merges = leaf_count.bit_length() - 1
    leaf_index = lax.axis_index("leaf")
    collected = []
    samples = lax.psum_scatter(
        lax.dot_general(
            sample_matrix, front_rows, (((0,), (1,)), ((), ())), preferred_element_type=jnp.float32
        ),
        "grp",
        scatter_dimension=0,
        tiled=True,
    )
    skeleton = samples
    for depth_level in range(merges + 1):
        offset = 2 * leaf_count - (2 * leaf_count >> depth_level)
        node_index = offset + (leaf_index >> depth_level)
        chosen = lax.dynamic_index_in_dim(pivots, node_index, 0, keepdims=False)
        skeleton = jnp.take(samples, chosen, axis=1)
        gram = lax.psum(contract_first(skeleton, skeleton), "grp")
        block = samples
        cross = lax.psum_scatter(
            contract_first(block, skeleton), "grp", scatter_dimension=0, tiled=True
        )
        collected.append(basis_from(gram, cross))
        if depth_level < merges:
            partner = from_partner(skeleton, "leaf", depth_level)
            which_side = (leaf_index >> depth_level) % 2
            lower_half = jnp.where(which_side == 0, skeleton, partner)
            upper_half = jnp.where(which_side == 0, partner, skeleton)
            samples = jnp.concatenate([lower_half, upper_half], axis=1)
    return (jnp.stack(collected)[:, None], skeleton)


def solution(mesh):
    placed = (P("leaf", "grp"), P("grp", None), P())
    return jax.shard_map(
        on_device,
        mesh=mesh,
        in_specs=placed,
        out_specs=(P(None, "leaf", "grp", None), P("grp", None)),
        check_vma=False,
    )
```

profile of v0, /device:TPU:30, one launch (start us, length us, event | category | flops | bytes accessed | tf_op | source)
XLA Modules:
  0.0 1056.0 jit_solution(7323625996431687745)
XLA Ops:
  17.1 83.0 %reduce-scatter.7.cloned.1.call-done = f32[64,1024]{1,0:T(8,128)} async-done(((f32[1024,1024]{1,0:T(8,128)}), f32[64,1024]{1,0:T(8,128)}) %reduce-scatter.7.cloned.1.call-update) | async-done | bytes 262160 | tf_op jit(solution)/shard_map/reduce_scatter | solution.py:41
  120.8 9.8 collective-permute-done.2
  139.8 10.1 collective-permute-done.3
  173.8 102.5 %all-reduce.4.cloned.1.call-done = (f32[512,512]{0,1:T(8,128)}, f32[512,512]{0,1:T(8,128)}, f32[512,512]{0,1:T(8,128)}, f32[512,512]{0,1:T(8,128)}, f32[512,512]{0,1:T(8,128)}) async-done(((f32[512,512]{0,1:T(8,128)}, f32[512,512]{0,1:T(8,128)}, f32[512,512]{0,1:T(8,128)}, f32[512,512]{0,1:T(8,128)}, f32[512,512]{0,1:T(8,128)}), (f32[512,512]{0,1:T(8,128)}, f32[512,512]{0,1:T(8,128)}, f32[512,512]{0,1:T(8,128)}, ...) | async-done | bytes 5242896 | tf_op jit(solution)/shard_map/psum | solution.py:55
  285.5 11.7 %cholesky.838 = f32[128,128]{1,0:T(8,128)S(1)} custom-call(f32[128,128]{1,0:T(8,128)S(1)} %cholesky.958), custom_call_target="Cholesky" | custom-call | tf_op jit(solution)/shard_map/jit(cholesky)/cholesky | solution.py:22
  297.4 9.8 custom-call.55
  309.8 20.5 %cholesky.857 = f32[128,128]{1,0:T(8,128)S(1)} custom-call(f32[128,128]{1,0:T(8,128)S(1)} %cholesky.962), custom_call_target="Cholesky" | custom-call | tf_op jit(solution)/shard_map/jit(cholesky)/cholesky | solution.py:22
  331.6 9.8 custom-call.56
  343.0 11.7 %cholesky.878 = f32[128,128]{1,0:T(8,128)S(1)} custom-call(f32[128,128]{1,0:T(8,128)S(1)} %cholesky.967), custom_call_target="Cholesky" | custom-call | tf_op jit(solution)/shard_map/jit(cholesky)/cholesky | solution.py:22
  355.5 9.8 custom-call.57
  366.7 12.1 %cholesky.895 = f32[128,128]{1,0:T(8,128)S(1)} custom-call(f32[128,128]{1,0:T(8,128)S(1)} %convolution_subtract_fusion.25), custom_call_target="Cholesky" | custom-call | tf_op jit(solution)/shard_map/jit(cholesky)/cholesky | solution.py:22
  382.3 8.2 while.14
  390.5 39.3 %custom-call.58 = f32[4,128,128]{1,2,0:T(8,128)S(1)} custom-call(f32[4,128,128]{2,1,0:T(8,128)S(1)} %get-tuple-element.41), custom_call_target="InvertDiagBlocksLowerTriangular" | custom-call | tf_op jit(solution)/shard_map/jit(_solve_triangular)/triangular_solve | solution.py:24
  436.7 11.7 %cholesky.766 = f32[128,128]{1,0:T(8,128)S(1)} custom-call(f32[128,128]{1,0:T(8,128)S(1)} %cholesky.945), custom_call_target="Cholesky" | custom-call | tf_op jit(solution)/shard_map/jit(cholesky)/cholesky | solution.py:22
  448.5 9.8 custom-call.51
  460.9 11.9 %cholesky.785 = f32[128,128]{1,0:T(8,128)S(1)} custom-call(f32[128,128]{1,0:T(8,128)S(1)} %cholesky.949), custom_call_target="Cholesky" | custom-call | tf_op jit(solution)/shard_map/jit(cholesky)/cholesky | solution.py:22
  474.2 9.8 custom-call.52
  485.6 11.7 %cholesky.806 = f32[128,128]{1,0:T(8,128)S(1)} custom-call(f32[128,128]{1,0:T(8,128)S(1)} %cholesky.954), custom_call_target="Cholesky" | custom-call | tf_op jit(solution)/shard_map/jit(cholesky)/cholesky | solution.py:22
  498.0 9.8 custom-call.53
  509.7 11.7 %cholesky.823 = f32[128,128]{1,0:T(8,128)S(1)} custom-call(f32[128,128]{1,0:T(8,128)S(1)} %convolution_subtract_fusion.26), custom_call_target="Cholesky" | custom-call | tf_op jit(solution)/shard_map/jit(cholesky)/cholesky | solution.py:22
  524.9 8.2 while.13
  533.1 39.3 %custom-call.54 = f32[4,128,128]{1,2,0:T(8,128)S(1)} custom-call(f32[4,128,128]{2,1,0:T(8,128)S(1)} %get-tuple-element.40), custom_call_target="InvertDiagBlocksLowerTriangular" | custom-call | tf_op jit(solution)/shard_map/jit(_solve_triangular)/triangular_solve | solution.py:24
  586.2 11.7 %cholesky.694 = f32[128,128]{1,0:T(8,128)S(1)} custom-call(f32[128,128]{1,0:T(8,128)S(1)} %cholesky.932), custom_call_target="Cholesky" | custom-call | tf_op jit(solution)/shard_map/jit(cholesky)/cholesky | solution.py:22
  598.1 9.8 custom-call.47
  610.6 11.7 %cholesky.713 = f32[128,128]{1,0:T(8,128)S(1)} custom-call(f32[128,128]{1,0:T(8,128)S(1)} %cholesky.936), custom_call_target="Cholesky" | custom-call | tf_op jit(solution)/shard_map/jit(cholesky)/cholesky | solution.py:22
  623.8 9.8 custom-call.48
  635.1 11.7 %cholesky.734 = f32[128,128]{1,0:T(8,128)S(1)} custom-call(f32[128,128]{1,0:T(8,128)S(1)} %cholesky.941), custom_call_target="Cholesky" | custom-call | tf_op jit(solution)/shard_map/jit(cholesky)/cholesky | solution.py:22
  647.5 10.0 custom-call.49
  659.0 11.7 %cholesky.751 = f32[128,128]{1,0:T(8,128)S(1)} custom-call(f32[128,128]{1,0:T(8,128)S(1)} %convolution_subtract_fusion.27), custom_call_target="Cholesky" | custom-call | tf_op jit(solution)/shard_map/jit(cholesky)/cholesky | solution.py:22
  681.3 39.7 %custom-call.50 = f32[4,128,128]{1,2,0:T(8,128)S(1)} custom-call(f32[4,128,128]{2,1,0:T(8,128)S(1)} %get-tuple-element.39), custom_call_target="InvertDiagBlocksLowerTriangular" | custom-call | tf_op jit(solution)/shard_map/jit(_solve_triangular)/triangular_solve | solution.py:24
  725.8 11.7 %cholesky.622 = f32[128,128]{1,0:T(8,128)S(1)} custom-call(f32[128,128]{1,0:T(8,128)S(1)} %cholesky.919), custom_call_target="Cholesky" | custom-call | tf_op jit(solution)/shard_map/jit(cholesky)/cholesky | solution.py:22
  737.7 9.8 custom-call.43
  750.0 11.9 %cholesky.641 = f32[128,128]{1,0:T(8,128)S(1)} custom-call(f32[128,128]{1,0:T(8,128)S(1)} %cholesky.923), custom_call_target="Cholesky" | custom-call | tf_op jit(solution)/shard_map/jit(cholesky)/cholesky | solution.py:22
  763.2 9.8 custom-call.44
  775.3 13.2 %cholesky.662 = f32[128,128]{1,0:T(8,128)} custom-call(f32[128,128]{1,0:T(8,128)} %cholesky.928), custom_call_target="Cholesky" | custom-call | tf_op jit(solution)/shard_map/jit(cholesky)/cholesky | solution.py:22
  790.7 11.3 %custom-call.45 = f32[1,128,128]{1,2,0:T(8,128)} custom-call(f32[1,128,128]{2,1,0:T(8,128)} %get-tuple-element.140), custom_call_target="InvertDiagBlocksLowerTriangular" | custom-call | tf_op jit(solution)/shard_map/jit(cholesky)/cholesky | solution.py:22
  804.2 12.1 %cholesky.679 = f32[128,128]{1,0:T(8,128)S(1)} custom-call(f32[128,128]{1,0:T(8,128)S(1)} %convolution_subtract_fusion.28), custom_call_target="Cholesky" | custom-call | tf_op jit(solution)/shard_map/jit(cholesky)/cholesky | solution.py:22
  820.6 11.7 %while.11 = (s32[]{:T(128)}, f32[512,512]{1,0:T(8,128)}, s32[4,2]{0,1:T(2,128)S(1)}, f32[4,128,128]{2,1,0:T(8,128)S(1)}, s32[]{:T(128)}) while((s32[]{:T(128)}, f32[512,512]{1,0:T(8,128)}, s32[4,2]{0,1:T(2,128)S(1)}, f32[4,128,128]{2,1,0:T(8,128)S(1)}, s32[]{:T(128)}) %tuple.162), condition=%wide.while_cond.clone, body=%wide.while_body.clone.sunk | while | flops 2 | bytes 131181 | solution.py:24
  832.4 39.3 %custom-call.46 = f32[4,128,128]{1,2,0:T(8,128)S(1)} custom-call(f32[4,128,128]{2,1,0:T(8,128)S(1)} %get-tuple-element.38), custom_call_target="InvertDiagBlocksLowerTriangular" | custom-call | tf_op jit(solution)/shard_map/jit(_solve_triangular)/triangular_solve | solution.py:24
  875.7 11.7 %cholesky.550 = f32[128,128]{1,0:T(8,128)S(1)} custom-call(f32[128,128]{1,0:T(8,128)S(1)} %cholesky.906), custom_call_target="Cholesky" | custom-call | tf_op jit(solution)/shard_map/jit(cholesky)/cholesky | solution.py:22
  887.6 9.8 custom-call.39
  900.0 11.7 %cholesky.569 = f32[128,128]{1,0:T(8,128)S(1)} custom-call(f32[128,128]{1,0:T(8,128)S(1)} %cholesky.910), custom_call_target="Cholesky" | custom-call | tf_op jit(solution)/shard_map/jit(cholesky)/cholesky | solution.py:22
  911.8 10.0 custom-call.40
  923.3 11.7 %cholesky.590 = f32[128,128]{1,0:T(8,128)S(1)} custom-call(f32[128,128]{1,0:T(8,128)S(1)} %cholesky.915), custom_call_target="Cholesky" | custom-call | tf_op jit(solution)/shard_map/jit(cholesky)/cholesky | solution.py:22
  935.7 9.8 custom-call.41
  947.0 11.9 %cholesky.607 = f32[128,128]{1,0:T(8,128)S(1)} custom-call(f32[128,128]{1,0:T(8,128)S(1)} %convolution_subtract_fusion.29), custom_call_target="Cholesky" | custom-call | tf_op jit(solution)/shard_map/jit(cholesky)/cholesky | solution.py:22
  964.2 12.0 %while.10 = (s32[]{:T(128)}, f32[512,512]{1,0:T(8,128)}, s32[4,2]{0,1:T(2,128)S(1)}, f32[4,128,128]{2,1,0:T(8,128)S(1)}, s32[]{:T(128)}) while((s32[]{:T(128)}, f32[512,512]{1,0:T(8,128)}, s32[4,2]{0,1:T(2,128)S(1)}, f32[4,128,128]{2,1,0:T(8,128)S(1)}, s32[]{:T(128)}) %tuple.163), condition=%wide.while_cond, body=%wide.while_body.sunk | while | flops 2 | bytes 131181 | solution.py:24
  980.1 39.3 %custom-call.42 = f32[4,128,128]{1,2,0:T(8,128)S(1)} custom-call(f32[4,128,128]{2,1,0:T(8,128)S(1)} %get-tuple-element.37), custom_call_target="InvertDiagBlocksLowerTriangular" | custom-call | tf_op jit(solution)/shard_map/jit(_solve_triangular)/triangular_solve | solution.py:24
  (336 shorter events, 237.4 us)
Async XLA Ops:
  7.2 1.9 copy-start
  7.2 93.0 %reduce-scatter.7.cloned.1.call-start = ((), (), s32[]{:S(2)}) async-start(), calls=%async_computation.6 | async-start | bytes 4456448 | tf_op jit(solution)/shard_map/reduce_scatter | solution.py:41
  16.0 260.3 %all-reduce.4.cloned.1.call-start = ((), (), s32[]{:S(2)}) async-start(), calls=%async_computation.12 | async-start | bytes 10485760 | tf_op jit(solution)/shard_map/psum | solution.py:55
  102.5 2.1 collective-permute-start
  106.0 8.8 collective-permute-start.1
  116.1 14.5 %collective-permute-start.2 = (f32[64,512]{0,1:T(8,128)S(1)}, f32[64,512]{0,1:T(8,128)S(1)}, u32[]{:S(2)}, u32[]{:S(2)}) collective-permute-start(f32[64,512]{0,1:T(8,128)S(1)} %select_bitcast_fusion.2), channel_id=1, source_target_pairs={{0,64},{16,80},{32,96},{48,112},{64,0},{80,16},{96,32},{112,48},{1... | collective-permute-start | bytes 393224 | tf_op jit(solution)/shard_map/ppermute | solution.py:8
  131.8 8.0 copy-start.17
  132.0 17.9 %collective-permute-start.3 = (f32[64,512]{0,1:T(8,128)S(1)}, f32[64,512]{0,1:T(8,128)S(1)}, u32[]{:S(2)}, u32[]{:S(2)}) collective-permute-start(f32[64,512]{0,1:T(8,128)S(1)} %select_bitcast_fusion.1), channel_id=1, source_target_pairs={{0,128},{16,144},{32,160},{48,176},{64,192},{80,208},{96,224},{112... | collective-permute-start | bytes 393224 | tf_op jit(solution)/shard_map/ppermute | solution.py:8
  150.9 0.7 copy-start.15
  154.4 2.3 copy-start.18
  156.4 878.7 %reduce-scatter.9.cloned.1.call-start = ((), (), s32[]{:S(2)}) async-start(), calls=%async_computation.7 | async-start | bytes 2228224 | tf_op jit(solution)/shard_map/reduce_scatter | solution.py:57
  160.0 877.9 %reduce-scatter.11.cloned.1.call-start = ((), (), s32[]{:S(2)}) async-start(), calls=%async_computation.8 | async-start | bytes 2228224 | tf_op jit(solution)/shard_map/reduce_scatter | solution.py:57
  163.2 877.4 %reduce-scatter.13.cloned.1.call-start = ((), (), s32[]{:S(2)}) async-start(), calls=%async_computation.9 | async-start | bytes 2228224 | tf_op jit(solution)/shard_map/reduce_scatter | solution.py:57
  166.4 4.2 copy-start.16
  166.4 876.9 %reduce-scatter.15.cloned.1.call-start = ((), (), s32[]{:S(2)}) async-start(), calls=%async_computation.10 | async-start | bytes 2228224 | tf_op jit(solution)/shard_map/reduce_scatter | solution.py:57
  169.6 876.4 %reduce-scatter.17.cloned.1.call-start = ((), (), s32[]{:S(2)}) async-start(), calls=%async_computation.11 | async-start | bytes 2228224 | tf_op jit(solution)/shard_map/reduce_scatter | solution.py:57
  276.3 5.3 copy-start.5
  276.3 5.3 copy-start.6
  284.6 1.0 copy-start.11
  533.1 41.0 %copy-start.9 = (f32[512,512]{1,0:T(8,128)}, f32[512,512]{1,0:T(8,128)S(1)}, u32[]{:S(2)}) copy-start(f32[512,512]{1,0:T(8,128)S(1)} %get-tuple-element.445) | copy-start | bytes 3145732
  573.7 6.0 copy-start.4
  574.5 6.4 copy-start.3
  585.3 1.0 copy-start.12
  722.3 27.7 %copy-start.13 = (f32[128,512]{1,0:T(8,128)}, f32[128,512]{1,0:T(8,128)S(1)}, u32[]{:S(2)}) copy-start(f32[128,512]{1,0:T(8,128)S(1)} %fusion.156) | copy-start | bytes 786436
  723.2 14.5 %copy-start.20 = (f32[128,512]{1,0:T(8,128)}, f32[128,512]{1,0:T(8,128)S(1)}, u32[]{:S(2)}) copy-start(f32[128,512]{1,0:T(8,128)S(1)} %fusion.154) | copy-start | bytes 786436
  773.3 100.8 %copy-start.2 = (f32[512,512]{0,1:T(8,128)S(1)}, f32[512,512]{0,1:T(8,128)}, u32[]{:S(2)}) copy-start(f32[512,512]{0,1:T(8,128)} %get-tuple-element.84) | copy-start | bytes 3145732
  871.7 2.4 copy-start.22
  872.2 2.0 copy-start.7
  874.7 1.0 copy-start.10
  898.7 77.5 %copy-start.14 = (f32[128,512]{1,0:T(8,128)S(1)}, f32[128,512]{1,0:T(8,128)}, u32[]{:S(2)}) copy-start(f32[128,512]{1,0:T(8,128)} %copy-done.13) | copy-start | bytes 786436
  898.7 77.5 %copy-start.21 = (f32[128,512]{1,0:T(8,128)S(1)}, f32[128,512]{1,0:T(8,128)}, u32[]{:S(2)}) copy-start(f32[128,512]{1,0:T(8,128)} %copy-done.20) | copy-start | bytes 786436
  945.6 73.8 %copy-start.19 = (f32[128,512]{1,0:T(8,128)S(1)}, f32[128,512]{1,0:T(8,128)}, u32[]{:S(2)}) copy-start(f32[128,512]{1,0:T(8,128)} %convolution_subtract_fusion.7) | copy-start | bytes 786436
  958.9 60.9 %copy-start.8 = (f32[128,512]{1,0:T(8,128)S(1)}, f32[128,512]{1,0:T(8,128)}, u32[]{:S(2)}) copy-start(f32[128,512]{1,0:T(8,128)} %copy-done.7) | copy-start | bytes 786436
  964.1 55.2 %copy-start.23 = (f32[4,128,128]{1,2,0:T(8,128)S(1)}, f32[4,128,128]{1,2,0:T(8,128)}, u32[]{:S(2)}) copy-start(f32[4,128,128]{1,2,0:T(8,128)} %copy-done.22) | copy-start | bytes 786436
  1032.2 16.5 %copy-start.1 = (bf16[1536,1024]{1,0:T(8,128)(2,1)S(1)}, bf16[1536,1024]{1,0:T(8,128)(2,1)}, u32[]{:S(2)}) copy-start(bf16[1536,1024]{1,0:T(8,128)(2,1)} %param.9) | copy-start | bytes 9437188
Sparse Core Ops, SparseCore 0:
  16.1 84.0 reduce-scatter.6
  156.6 119.6 all-reduce.3
  279.8 80.3 reduce-scatter.8
  363.6 80.1 reduce-scatter.10
  447.2 80.1 reduce-scatter.12
  530.9 80.0 reduce-scatter.14
  614.5 80.1 reduce-scatter.16
where the time goes:
time: 1070 us; the launch traced here: 1060 us
  other arithmetic  619 us (58%)
  waiting for transfers between devices  211 us (20%)
  matrix products  114 us (11%)
  local copies, waits for them, and re-layouts  72.5 us (7%)
  between operations  28.7 us (3%)
    another operation x74, other arithmetic, basis_from(): factor = jnp.linalg.cholesky(gram)  410 us
    another operation x11, other arithmetic, basis_from(): jax.scipy.linalg.solve_triangular(factor, identity, lower=True)  200 us
    psum x1, waiting for transfers between devices, on_device(): gram = lax.psum(contract_first(skeleton, skeleton), 'grp')  102 us
    reduce_scatter x1, waiting for transfers between devices, on_device(): lax.psum_scatter(lax.dot_general(sample_matrix, front_rows, (((0,), (1,))...  83 us
    another operation x66, local copies, waits for them, and re-layouts, basis_from(): jax.scipy.linalg.solve_triangular(factor, identity, lower=True)  47.2 us
    another operation x30, matrix products, basis_from(): factor = jnp.linalg.cholesky(gram)  28.9 us
    dot_general x10, matrix products, contract_first(): lax.dot_general(left_side, right_side, (((0,), (0,)), ((), ())), precisio...  25.8 us
    ppermute x4, waiting for transfers between devices, from_partner(): lax.ppermute(x, axis, [(i, i ^ 1 << bit) for i in range(lax.axis_size(axi...  25 us
  transfers between devices with their start and end apart: 11, of which 5 were waited for; matrix products, arithmetic and copies ran while one was open for 74% of the time, Pallas kernels for 0%

commit v1 on v0

v1 whole, which is shorter than its diff:
```python
import jax
import jax.numpy as jnp
from jax import lax
from jax.experimental import pallas as pl
from jax.experimental.pallas import tpu as pltpu
from jax.sharding import PartitionSpec as P

HI = lax.Precision.HIGHEST
MESH = pl.DeviceIdType.MESH
SOLVERS = ((0, 0, 0), (0, 1, 10), (1, 0, 2), (2, 1, 8), (3, 0, 5), (4, 1, 15))


def bit(value, place):
    return lax.rem(value // (1 << place), 2)


def flip(value, mask):
    for place in range(4):
        if mask >> place & 1:
            value = value + (1 << place) * (1 - 2 * bit(value, place))
    return value


def send(src, dst, send_sem, recv_sem, device):
    return pltpu.make_async_remote_copy(
        src_ref=src, dst_ref=dst, send_sem=send_sem, recv_sem=recv_sem, device_id=device, device_id_type=MESH
    )


def permuted(src, index):
    rows = src.shape[0]
    wanted = jnp.where(lax.broadcasted_iota(jnp.int32, (256, 256), 0) == index, 1.0, 0.0).astype(jnp.bfloat16)
    high = src.astype(jnp.bfloat16)
    rest = src - high.astype(jnp.float32)
    middle = rest.astype(jnp.bfloat16)
    low = (rest - middle.astype(jnp.float32)).astype(jnp.bfloat16)
    stacked = jnp.concatenate([high, middle, low], axis=0)
    out = jnp.dot(stacked, wanted, preferred_element_type=jnp.float32)
    return (out[:rows] + out[rows : 2 * rows]) + out[2 * rows :]


def gather_kernel(
    p_ref, index_ref, z_ref, top_ref,
    hop1, comb1, near1, sum1, hop2, comb2, near2, y_ref, a3_ref, r1_ref, r2_ref, r3_ref, r4_ref,
    rs_send, rs_recv, leaf_send, leaf_recv, z_send, z_recv, z_local,
):
    leaf, grp = lax.axis_index("leaf"), lax.axis_index("grp")
    y, x = grp // 4, lax.rem(grp, 4)
    core = lax.rem(leaf, 2)

    barrier = pltpu.get_barrier_semaphore()
    for other in range(1, 16):
        pl.semaphore_signal(barrier, inc=1, device_id=(leaf, lax.rem(grp + other, 16)), device_id_type=MESH)
        pl.semaphore_signal(barrier, inc=1, device_id=(lax.rem(leaf + other, 16), grp), device_id_type=MESH)
    pl.semaphore_wait(barrier, 30)

    started = []

    def begin(copy):
        copy.start()
        started.append(copy)
        return copy

    def neighbour(along_x, offset):
        if along_x:
            return (leaf, y * 4 + lax.rem(x + offset, 4))
        return (leaf, lax.rem(y + offset, 4) * 4 + x)

    def source(phase, half, chunk, sub):
        if phase == 0:
            lanes = pl.ds(512 * half, 512)
            if half == 0:
                return p_ref.at[pl.ds(2 * sub, 2), chunk, :, lanes]
            return p_ref.at[chunk, pl.ds(2 * sub, 2), :, lanes]
        return sum1.at[half, chunk, pl.ds(32 * sub, 32), :]

    def landing(phase, half, way, sub):
        if phase == 0:
            return near1.at[half, way, pl.ds(2 * sub, 2), :, :]
        return near2.at[half, way, pl.ds(32 * sub, 32), :]

    hops, combs = (hop1, hop2), (comb1, comb2)
    rings = {}

    def ring_first(phase, half):
        along_x = (phase == 0) == (half == 0)
        at = x if along_x else y
        for way in range(2):
            to = neighbour(along_x, 1 if way == 0 else 3)
            sems = lambda kind: (rs_send.at[phase, half, way, kind], rs_recv.at[phase, half, way, kind])
            rings[phase, half, way, 0] = begin(
                send(source(phase, half, lax.rem(at + 2, 4), way), hops[phase].at[half, way], *sems(0), to)
            )
        for way in range(2):
            to = neighbour(along_x, 1 if way == 0 else 3)
            sems = lambda kind: (rs_send.at[phase, half, way, kind], rs_recv.at[phase, half, way, kind])
            chunk = lax.rem(at + (1 if way == 0 else 3), 4)
            rings[phase, half, way, 1] = begin(
                send(source(phase, half, chunk, 1 - way), landing(phase, half, way, 1 - way), *sems(1), to)
            )

    def ring_second(phase, half):
        along_x = (phase == 0) == (half == 0)
        at = x if along_x else y
        for way in range(2):
            to = neighbour(along_x, 1 if way == 0 else 3)
            chunk = lax.rem(at + (1 if way == 0 else 3), 4)
            rings[phase, half, way, 0].wait_recv()
            combs[phase][half, way] = hops[phase][half, way] + source(phase, half, chunk, way)[...]
            rings[phase, half, way, 2] = begin(
                send(
                    combs[phase].at[half, way], landing(phase, half, way, way),
                    rs_send.at[phase, half, way, 2], rs_recv.at[phase, half, way, 2], to,
                )
            )

    def ring_last(phase, half):
        for way in range(2):
            for kind in (1, 2):
                rings[phase, half, way, kind].wait_recv()

    for half in range(2):
        ring_first(0, half)
    for half in range(2):
        ring_second(0, half)
    for half in range(2):
        ring_last(0, half)
        if half == 0:
            own = p_ref[:, x, :, 0:512]
        else:
            own = p_ref[y, :, :, 512:1024]
        sum1[half] = (near1[half, 0] + own) + near1[half, 1]
        ring_first(1, half)
    for half in range(2):
        ring_second(1, half)
    mine = []
    for half in range(2):
        ring_last(1, half)
        own = sum1[half, y if half == 0 else x]
        mine.append((near2[half, 0] + own) + near2[half, 1])

    def select(level, block, value):
        chosen = permuted(value, index_ref[level * 4 + block])
        y_ref[level, block] = chosen[:, :128]
        y_ref[level, block + 4] = chosen[:, 128:]

    def pair(ref, *place):
        return jnp.concatenate([ref[place[:-1] + (place[-1],)], ref[place[:-1] + (place[-1] + 1,)]], axis=1)

    def to_solver(level):
        for of_level, of_core, place in SOLVERS:
            if of_level != level:
                continue
            is_core = core == of_core

            @pl.when(jnp.logical_and(is_core, grp != place))
            def _():
                send(y_ref.at[level], z_ref.at[grp], z_send.at[level], z_recv.at[grp], (leaf, place)).start()

            @pl.when(jnp.logical_and(is_core, grp == place))
            def _():
                pltpu.make_async_copy(y_ref.at[level], z_ref.at[grp], z_local).start()

    def solver_end(level):
        for of_level, of_core, place in SOLVERS:
            if of_level != level:
                continue
            is_core = core == of_core

            @pl.when(jnp.logical_and(is_core, grp != place))
            def _():
                send(y_ref.at[level], z_ref.at[grp], z_send.at[level], z_recv.at[grp], (leaf, place)).wait_send()

            @pl.when(jnp.logical_and(is_core, grp == place))
            def _():
                pltpu.make_async_copy(y_ref.at[level], z_ref.at[grp], z_local).wait()
                for source_grp in range(16):
                    if source_grp != place:
                        send(
                            y_ref.at[level], z_ref.at[source_grp], z_send.at[level], z_recv.at[source_grp], (leaf, source_grp)
                        ).wait_recv()

    side = [bit(leaf, b) for b in range(4)]
    for block in range(4):
        select(0, block, mine[block // 2][:, 256 * (block % 2) : 256 * (block % 2) + 256])
    out1 = begin(send(y_ref.at[0, pl.ds(0, 4)], r1_ref, leaf_send.at[0], leaf_recv.at[0], (flip(leaf, 1), grp)))
    for i in range(2):
        select(1, 2 * side[0] + i, pair(y_ref, 0, 2 * i))
    out2 = []
    for m in (2, 3):
        out2.append(
            begin(
                send(
                    y_ref.at[1, pl.ds(2 * side[0], 2)], r2_ref.at[lax.rem(leaf, 2)],
                    leaf_send.at[m - 1], leaf_recv.at[1 + lax.rem(leaf, 2)], (flip(leaf, m), grp),
                )
            )
        )
    own2 = 2 * side[1] + side[0]
    select(2, own2, pair(y_ref, 1, 2 * side[0]))
    for m in range(4, 8):
        begin(
            send(
                y_ref.at[2, own2], r3_ref.at[lax.rem(leaf, 4)],
                leaf_send.at[m - 1], leaf_recv.at[3 + lax.rem(leaf, 4)], (flip(leaf, m), grp),
            )
        )
    own3 = 2 * side[2] + side[1]
    value = y_ref[2, own2]
    zero = jnp.zeros_like(value)
    wide = jnp.concatenate([jnp.where(side[0] == 0, value, zero), jnp.where(side[0] == 0, zero, value)], axis=1)
    placed = permuted(wide, index_ref[12 + own3])[:, :128]
    a3_ref[...] = placed[:32] + pltpu.roll(placed[32:], 64, 1)
    for m in range(8, 16):
        begin(
            send(
                a3_ref, r4_ref.at[lax.rem(leaf, 8)],
                leaf_send.at[m - 1], leaf_recv.at[7 + lax.rem(leaf, 8)], (flip(leaf, m), grp),
            )
        )
    to_solver(0)

    def arrived(ref, slot):
        send(ref, ref, leaf_send.at[0], leaf_recv.at[slot], (flip(leaf, 1), grp)).wait_recv()

    arrived(r1_ref, 0)
    for i in range(2):
        select(1, 2 * (1 - side[0]) + i, pair(r1_ref, 2 * i))
    to_solver(1)
    select(2, 2 * side[1] + 1 - side[0], pair(y_ref, 1, 2 * (1 - side[0])))
    for s in range(2):
        arrived(r2_ref.at[s], 1 + s)
    for s in range(2):
        select(2, 2 * (1 - side[1]) + s, jnp.concatenate([r2_ref[s, 0], r2_ref[s, 1]], axis=1))
    to_solver(2)
    for i in range(2):
        select(3, 2 * side[2] + i, pair(y_ref, 2, 2 * i))
    for s in range(4):
        arrived(r3_ref.at[s], 3 + s)
    for i in range(2):
        select(3, 2 * (1 - side[2]) + i, pair(r3_ref, 2 * i))
    to_solver(3)
    for i in range(2):
        select(4, 2 * side[3] + i, pair(y_ref, 3, 2 * i))
    for s in range(8):
        arrived(r4_ref.at[s], 7 + s)
    low_lanes = lax.broadcasted_iota(jnp.int32, (32, 128), 1) < 64
    joined = []
    for i in range(4):
        even, odd = r4_ref[2 * i], r4_ref[2 * i + 1]
        upper = jnp.where(low_lanes, even, odd)
        lower = pltpu.roll(jnp.where(low_lanes, odd, even), 64, 1)
        joined.append(jnp.concatenate([upper, lower], axis=0))
    for i in range(2):
        select(4, 2 * (1 - side[3]) + i, jnp.concatenate([joined[2 * i], joined[2 * i + 1]], axis=1))
    to_solver(4)
    for b in range(4):
        top_ref[:, 128 * b : 128 * b + 128] = y_ref[4, b]
    for copy in started:
        copy.wait_send()
    for level in range(5):
        solver_end(level)


def gathered(partial, index):
    dma = pltpu.SemaphoreType.DMA
    f32 = lambda *shape: pltpu.VMEM(shape, jnp.float32)
    return pl.pallas_call(
        gather_kernel,
        out_shape=(jax.ShapeDtypeStruct((16, 8, 64, 128), jnp.float32), jax.ShapeDtypeStruct((64, 512), jnp.float32)),
        in_specs=[pl.BlockSpec(memory_space=pltpu.VMEM)] * 2,
        out_specs=(pl.BlockSpec(memory_space=pl.ANY), pl.BlockSpec(memory_space=pltpu.VMEM)),
        scratch_shapes=[
            f32(2, 2, 2, 64, 512), f32(2, 2, 2, 64, 512), f32(2, 2, 4, 64, 512), f32(2, 4, 64, 512),
            f32(2, 2, 32, 512), f32(2, 2, 32, 512), f32(2, 2, 64, 512),
            f32(5, 8, 64, 128), f32(32, 128), f32(4, 64, 128), f32(2, 2, 64, 128), f32(4, 64, 128), f32(8, 32, 128),
            dma((2, 2, 2, 3)), dma((2, 2, 2, 3)), dma((15,)), dma((15,)), dma((5,)), dma((16,)), dma,
        ],
        compiler_params=pltpu.CompilerParams(collective_id=1, has_side_effects=True, vmem_limit_bytes=56 * 1024 * 1024),
    )(partial, index)


def spread_kernel(u_ref, pivot_ref, other_ref, out_ref, rows_ref, u_send, u_recv, u_local):
    leaf, grp = lax.axis_index("leaf"), lax.axis_index("grp")
    core = lax.rem(leaf, 2)
    base = leaf - core
    barrier = pltpu.get_barrier_semaphore()
    for other in range(1, 16):
        pl.semaphore_signal(barrier, inc=1, device_id=(leaf, lax.rem(grp + other, 16)), device_id_type=MESH)
    for other in range(16):
        pl.semaphore_signal(barrier, inc=1, device_id=(base + 1 - core, other), device_id_type=MESH)
    pl.semaphore_wait(barrier, 31)

    def each(level, of_core, place, act):
        def to(target_core, target, slot):
            return send(
                u_ref.at[pl.ds(32 * target, 32)], rows_ref.at[level], u_send.at[slot], u_recv.at[level],
                (base + target_core, target),
            )

        @pl.when(jnp.logical_and(core == of_core, grp == place))
        def _():
            for target in range(16):
                if target != place:
                    act(to(of_core, target, target))
                if level > 0:
                    act(to(1 - of_core, target, 16 + target))

    for level, of_core, place in SOLVERS:
        each(level, of_core, place, lambda copy: copy.start())

    for level, of_core, place in SOLVERS:
        own = jnp.logical_and(core == of_core, grp == place)

        @pl.when(own)
        def _():
            copy = pltpu.make_async_copy(u_ref.at[pl.ds(32 * place, 32)], rows_ref.at[level], u_local)
            copy.start()
            copy.wait()

        gets = jnp.logical_not(own)
        if level == 0:
            gets = jnp.logical_and(core == of_core, gets)

        @pl.when(gets)
        def _():
            send(
                u_ref.at[pl.ds(0, 32)], rows_ref.at[level], u_send.at[0], u_recv.at[level], (base + of_core, place)
            ).wait_recv()

    for level in range(5):
        at = grp * 64 + lax.broadcasted_iota(jnp.int32, (64, 512), 0)
        is_pivot = jnp.where(at == pivot_ref[level], 1.0, 0.0)
        spot = jnp.where(lax.broadcasted_iota(jnp.int32, (64, 32), 0) == other_ref[level], 1.0, 0.0)
        rest = lax.dot_general(
            spot, rows_ref[level], (((1,), (0,)), ((), ())), precision=HI, preferred_element_type=jnp.float32
        )
        out_ref[level] = is_pivot + rest
    for level, of_core, place in SOLVERS:
        each(level, of_core, place, lambda copy: copy.wait_send())


def spread(u, pivot, other):
    dma = pltpu.SemaphoreType.DMA
    return pl.pallas_call(
        spread_kernel,
        out_shape=jax.ShapeDtypeStruct((5, 64, 512), jnp.float32),
        in_specs=[pl.BlockSpec(memory_space=pltpu.VMEM)] * 3,
        out_specs=pl.BlockSpec(memory_space=pltpu.VMEM),
        scratch_shapes=[pltpu.VMEM((5, 32, 512), jnp.float32), dma((32,)), dma((5,)), dma],
        compiler_params=pltpu.CompilerParams(collective_id=2, has_side_effects=True, vmem_limit_bytes=16 * 1024 * 1024),
    )(u, pivot, other)


def is_solver():
    leaf, grp = lax.axis_index("leaf"), lax.axis_index("grp")
    core = lax.rem(leaf, 2)
    found = False
    for _, of_core, place in SOLVERS:
        found = jnp.logical_or(found, jnp.logical_and(core == of_core, grp == place))
    return found


def invert(read):
    lane = lax.broadcasted_iota(jnp.int32, (8, 128), 1)
    sub = lax.broadcasted_iota(jnp.int32, (8, 128), 0)

    def eight(_, blocks):
        blocks = list(blocks)
        for s in range(8):
            row = blocks[0][s : s + 1, :]
            scale = 1.0 / row[:, s : s + 1]
            scaled = jnp.where(lane[:1] == s, scale, row * scale)
            for i in range(16):
                rest = jnp.where(lane == s, 0.0, blocks[i])
                new = rest - blocks[i][:, s : s + 1] * scaled
                if i == 0:
                    new = jnp.where(sub == s, scaled, new)
                blocks[i] = new
        blocks = [pltpu.roll(b, 120, 1) for b in blocks]
        return tuple(blocks[1:] + blocks[:1])

    blocks = tuple(read(i) for i in range(16))
    return jnp.concatenate(lax.fori_loop(0, 16, eight, blocks), axis=0)

def dot(a, b):
    return lax.dot_general(a, b, (((1,), (0,)), ((), ())), precision=HI, preferred_element_type=jnp.float32)

def solve_kernel(z_ref, u_ref, m_ref):
    step = pl.program_id(0)

    active = is_solver()

    @pl.when(step == 0)
    def _():
        m_ref[...] = jnp.zeros_like(m_ref)
    @pl.when(active)
    def _():
        rows = []
        for g in range(4):
            rows.append(jnp.concatenate([z_ref[g, b] for b in range(8)], axis=1))
        z = jnp.concatenate(rows, axis=0)
        m_ref[...] += lax.dot_general(z, z[:, :512], (((0,), (0,)), ((), ())), precision=HI, preferred_element_type=jnp.float32)

    @pl.when(jnp.logical_and(active, step == 3))
    def _():
        for p in range(4):
            at = 128 * p
            dinv = invert(lambda i: m_ref[at + 8 * i : at + 8 * i + 8, at : at + 128])
            lead = m_ref[at : at + 128, :]
            for low in range(at + 128, 1024, 128):
                w = dot(m_ref[low : low + 128, at : at + 128], dinv)
                for q in range(4):
                    if q != p:
                        m_ref[low : low + 128, 128 * q : 128 * q + 128] -= dot(w, lead[:, 128 * q : 128 * q + 128])
                m_ref[low : low + 128, at : at + 128] = w
        u_ref[...] = m_ref[512:, :]

def solve(z):
    return pl.pallas_call(
        solve_kernel,
        grid=(4,),
        in_specs=[pl.BlockSpec((4, 8, 64, 128), lambda i: (i, 0, 0, 0))],
        out_specs=pl.BlockSpec((512, 512), lambda i: (0, 0)),
        out_shape=jax.ShapeDtypeStruct((512, 512), jnp.float32),
        scratch_shapes=[pltpu.VMEM((1024, 512), jnp.float32)],
        compiler_params=pltpu.CompilerParams(dimension_semantics=("arbitrary",), vmem_limit_bytes=60 * 1024 * 1024),
    )(z)


def orders(pivots, leaf):
    nodes = jnp.stack([32 - (32 >> level) + leaf // (1 << level) for level in range(5)])
    chosen = jnp.take(pivots, nodes, axis=0)
    local = chosen.reshape(5, 16, 32) - 64 * jnp.arange(16, dtype=jnp.int32)[:, None]
    places = jnp.arange(64, dtype=jnp.int32)
    free = jnp.logical_not((local[:, :, :, None] == places).any(2))
    before = (free[:, :, None, :] & (places[None, :] < places[:, None])).sum(-1, dtype=jnp.int32)
    slots = jnp.arange(32, dtype=jnp.int32)[:, None]
    other = jnp.where(free[:, :, None, :] & (before[:, :, None, :] == slots), places, 0).sum(-1, dtype=jnp.int32)
    shift = 64 * (jnp.arange(16, dtype=jnp.int32) % 4)[:, None]
    index = jnp.concatenate([(local + shift).reshape(20, 1, 128), (other + shift).reshape(20, 1, 128)], axis=2)
    return chosen, other, index


def on_device(front_rows, sample_matrix, pivots):
    leaf, grp = lax.axis_index("leaf"), lax.axis_index("grp")
    chosen, other, index = orders(pivots, leaf)
    partial = lax.dot_general(
        sample_matrix, front_rows, (((0,), (1,)), ((), ())), preferred_element_type=jnp.float32
    ).reshape(4, 4, 64, 1024)
    z, top = gathered(partial, index)
    u = solve(z)
    mine = lax.dynamic_index_in_dim(other, grp, 1, keepdims=True)
    bases = spread(u, chosen[:, None, :], mine)
    return (bases[:, None], top)


def solution(mesh):
    return jax.shard_map(
        on_device,
        mesh=mesh,
        in_specs=(P("leaf", "grp"), P("grp", None), P()),
        out_specs=(P(None, "leaf", "grp", None), P("grp", None)),
        check_vma=False,
    )
```

time: 1070 us -> 176 us (0.16); the launches traced: 1060 us -> 175 us
  other arithmetic: 619 us -> 4.27 us
  waiting for transfers between devices: 211 us -> 0 us
  Pallas kernels: 0 us -> 158 us
  matrix products: 114 us -> 6.94 us
  local copies, waits for them, and re-layouts: 72.5 us -> 5.24 us
  between operations: 28.7 us -> 0.79 us
    another operation x85 -> x0, other arithmetic: 609 us -> none  [the longest x74 410 us: basis_from(): factor = jnp.linalg.cholesky(gram)]
    pallas_call x0 -> x3, Pallas kernels: none -> 158 us  [the longest x1 93.7 us: spread(): pl.pallas_call(spread_kernel, out_shape=jax.ShapeDtypeStruct((5, 64, 512)...]
    psum x1 -> x0, waiting for transfers between devices: 102 us -> none  [on_device(): gram = lax.psum(contract_first(skeleton, skeleton), 'grp')]
    reduce_scatter x6 -> x0, waiting for transfers between devices: 83 us -> none  [the longest x1 83 us: on_device(): lax.psum_scatter(lax.dot_general(sample_matrix, front_rows, (((0,), (1,))...]
    dot_general x20 -> x0, matrix products: 54.8 us -> none  [the longest x10 25.8 us: contract_first(): lax.dot_general(left_side, right_side, (((0,), (0,)), ((), ())), precisio...]
    another operation x65 -> x0, matrix products: 52.2 us -> none  [the longest x30 28.9 us: basis_from(): factor = jnp.linalg.cholesky(gram)]
    another operation x86 -> x2, local copies, waits for them, and re-layouts: 50.2 us -> 0.19 us  [orders(): jnp.stack([32 - (32 >> level) + leaf // (1 << level) for level in range(5)])]
    ppermute x4 -> x0, waiting for transfers between devices: 25 us -> none  [from_partner(): lax.ppermute(x, axis, [(i, i ^ 1 << bit) for i in range(lax.axis_size(axi...]
  transfers between devices with their start and end apart: 11 -> 0, of which waited for: 5 -> 0; matrix products, arithmetic and copies ran while one was open for 74% -> 0% of each run, Pallas kernels for 0% -> 0%
where the time goes in v1:
time: 176 us; the launch traced here: 175 us
  Pallas kernels  158 us (90%)
  matrix products  6.94 us (4%)
  local copies, waits for them, and re-layouts  5.24 us (3%)
  other arithmetic  4.27 us (2%)
    pallas_call x1, Pallas kernels, spread(): pl.pallas_call(spread_kernel, out_shape=jax.ShapeDtypeStruct((5, 64, 512)...  93.7 us
    pallas_call x1, Pallas kernels, gathered(): pl.pallas_call(gather_kernel, out_shape=(jax.ShapeDtypeStruct((16, 8, 64,...  60.4 us
    dot_general x1, matrix products, on_device(): lax.dot_general(sample_matrix, front_rows, (((0,), (1,)), ((), ())), pref...  6.94 us
    pallas_call x1, Pallas kernels, solve(): pl.pallas_call(solve_kernel, grid=(4,), in_specs=[pl.BlockSpec((4, 8, 64,...  4.11 us

profile of v1, /device:TPU:30, one launch (start us, length us, event | category | flops | bytes accessed | tf_op | source)
XLA Modules:
  0.0 175.5 jit_solution(6519386492308261849)
XLA Ops:
  0.6 0.0 copy-start
  0.7 0.1 stack.35
  0.8 0.1 stack.41
  0.9 0.1 broadcast_in_dim.43
  1.0 0.1 broadcast_in_dim.52
  1.1 1.6 gather_fusion
  2.8 0.1 broadcast_select_fusion.pivot_ref
  2.8 0.1 gather.12
  2.9 0.1 select_subtract_fusion
  3.0 0.6 fusion
  3.6 1.4 convert_reduce_fusion
  5.0 1.4 select_reduce_fusion
  6.5 0.1 reduce_sum.23
  6.5 0.1 sub.43
  6.6 0.1 sub.44
  6.7 0.1 add.78
  6.8 0.1 add.79
  6.9 0.6 pad_add_fusion.index_ref
  7.5 0.0 copy-done
  7.5 6.9 %fusion.4 = f32[1024,1024]{1,0:T(8,128)} fusion(bf16[1536,1024]{1,0:T(8,128)(2,1)S(1)} %copy-done, bf16[1024,1536]{1,0:T(8,128)(2,1)} %param.3), kind=kOutput, calls=%fused_computation.21 | convolution fusion | flops 3221225472 | bytes 10485760 | tf_op jit(solution)/shard_map/dot_general | solution.py:448
  14.5 60.4 %shard_map.50 = (f32[16,8,64,128]{3,2,1,0:T(8,128)}, f32[64,512]{1,0:T(8,128)}) custom-call(f32[4,4,64,1024]{3,2,1,0:T(8,128)} %bitcast.19, s32[20,1,256]{2,1,0:T(1,128)} %pad_add_fusion.index_ref), custom_call_target="tpu_custom_call" | custom-call | tf_op jit(solution)/shard_map/pallas_call | solution.py:268
  74.9 0.0 copy-start.2
  74.9 4.1 %shard_map.51.u_ref = f32[512,512]{1,0:T(8,128)} custom-call(f32[16,8,64,128]{3,2,1,0:T(8,128)} %get-tuple-element.4.z_ref), custom_call_target="tpu_custom_call" | custom-call | tf_op jit(solution)/shard_map/pallas_call | solution.py:420
  79.1 0.0 copy-start.1
  79.1 1.2 copy-done.1
  80.3 93.7 %shard_map.52 = f32[5,64,512]{2,1,0:T(8,128)S(1)} custom-call(f32[512,512]{1,0:T(8,128)S(1)} %copy-done.1, s32[5,1,512]{2,1,0:T(1,128)S(1)} %broadcast_select_fusion.pivot_ref, s32[5,1,32]{2,1,0:T(1,128)S(1)} %constant_dynamic-slice_fusion.other_ref), custom_call_target="tpu_custom_call" | custom-call | tf_op jit(solution)/shard_map/pallas_call | solution.py:345
  174.0 0.8 copy.15
  174.8 0.0 copy-done.2
  174.8 0.7 copy.16
  (10 shorter events, 0.1 us)
Async XLA Ops:
  0.6 6.9 %copy-start = (bf16[1536,1024]{1,0:T(8,128)(2,1)S(1)}, bf16[1536,1024]{1,0:T(8,128)(2,1)}, u32[]{:S(2)}) copy-start(bf16[1536,1024]{1,0:T(8,128)(2,1)} %param.4) | copy-start | bytes 9437188
  74.9 99.9 %copy-start.2 = (f32[64,512]{1,0:T(8,128)S(1)}, f32[64,512]{1,0:T(8,128)}, u32[]{:S(2)}) copy-start(f32[64,512]{1,0:T(8,128)} %get-tuple-element.17) | copy-start | bytes 393220
  79.1 1.2 copy-start.1

commit v2 on v1

--- a/solution.py
+++ b/solution.py
@@ -361,27 +361,51 @@
     return found
 
 
+def wide(value):
+    return jnp.broadcast_to(value, (8, 128))
+
+
+def small_inverse(columns, sub):
+    columns = list(columns)
+    for k in range(8):
+        rows = [wide(column[k : k + 1, :]) for column in columns]
+        scale = 1.0 / rows[k]
+        here = sub == k
+        lead = columns[k]
+        for j in range(8):
+            if j != k:
+                row = rows[j] * scale
+                columns[j] = jnp.where(here, row, columns[j] - lead * row)
+        columns[k] = jnp.where(here, scale, -(lead * scale))
+    return columns
+
+
+def weighted(columns, rows):
+    even, odd = columns[0] * rows[0], columns[1] * rows[1]
+    for j in range(2, 8, 2):
+        even = even + columns[j] * rows[j]
+        odd = odd + columns[j + 1] * rows[j + 1]
+    return even + odd
+
+
 def invert(read):
     lane = lax.broadcasted_iota(jnp.int32, (8, 128), 1)
     sub = lax.broadcasted_iota(jnp.int32, (8, 128), 0)
+    eye = jnp.where(lane == sub, 1.0, 0.0)
 
     def eight(_, blocks):
-        blocks = list(blocks)
-        for s in range(8):
-            row = blocks[0][s : s + 1, :]
-            scale = 1.0 / row[:, s : s + 1]
-            scaled = jnp.where(lane[:1] == s, scale, row * scale)
-            for i in range(16):
-                rest = jnp.where(lane == s, 0.0, blocks[i])
-                new = rest - blocks[i][:, s : s + 1] * scaled
-                if i == 0:
-                    new = jnp.where(sub == s, scaled, new)
-                blocks[i] = new
-        blocks = [pltpu.roll(b, 120, 1) for b in blocks]
-        return tuple(blocks[1:] + blocks[:1])
-
-    blocks = tuple(read(i) for i in range(16))
-    return jnp.concatenate(lax.fori_loop(0, 16, eight, blocks), axis=0)
+        corner = small_inverse([wide(blocks[0][:, 8 + j : 9 + j]) for j in range(8)], sub)
+        columns = [[wide(block[:, 8 + j : 9 + j]) for j in range(8)] for block in blocks[1:]]
+        rolled = [pltpu.roll(block, 120, 1) for block in blocks]
+        top = jnp.where(lane < 8, eye, rolled[0])
+        new = weighted(corner, [wide(top[j : j + 1]) for j in range(8)])
+        rows = [wide(new[j : j + 1]) for j in range(8)]
+        rest = [jnp.where(lane < 8, 0.0, block) - weighted(cols, rows) for cols, block in zip(columns, rolled[1:])]
+        return tuple(rest + [new])
+
+    blocks = lax.fori_loop(0, 16, eight, tuple(pltpu.roll(read(i), 8, 1) for i in range(16)))
+    return jnp.concatenate([pltpu.roll(block, 120, 1) for block in blocks], axis=0)
+
 
 def dot(a, b):
     return lax.dot_general(a, b, (((1,), (0,)), ((), ())), precision=HI, preferred_element_type=jnp.float32)

time: 176 us -> 149 us (0.85)
  Pallas kernels: 158 us -> 131 us
    pallas_call x1, Pallas kernels: 93.7 us -> 66.7 us  [spread(): pl.pallas_call(spread_kernel, out_shape=jax.ShapeDtypeStruct((5, 64, 512)...]
where the time goes in v2:
time: 149 us; the launch traced here: 148 us
  Pallas kernels  131 us (88%)
  matrix products  6.94 us (5%)
  local copies, waits for them, and re-layouts  5.24 us (4%)
  other arithmetic  4.27 us (3%)
    pallas_call x1, Pallas kernels, spread(): pl.pallas_call(spread_kernel, out_shape=jax.ShapeDtypeStruct((5, 64, 512)...  66.7 us
    pallas_call x1, Pallas kernels, gathered(): pl.pallas_call(gather_kernel, out_shape=(jax.ShapeDtypeStruct((16, 8, 64,...  60.4 us
    dot_general x1, matrix products, on_device(): lax.dot_general(sample_matrix, front_rows, (((0,), (1,)), ((), ())), pref...  6.94 us
    pallas_call x1, Pallas kernels, solve(): pl.pallas_call(solve_kernel, grid=(4,), in_specs=[pl.BlockSpec((4, 8, 64,...  4.11 us

profile of v2, /device:TPU:30, one launch (start us, length us, event | category | flops | bytes accessed | tf_op | source)
XLA Modules:
  0.0 148.4 jit_solution(17961378937101485307)
XLA Ops:
  0.6 0.0 copy-start
  0.7 0.1 stack.35
  0.8 0.1 stack.41
  0.9 0.1 broadcast_in_dim.43
  1.0 0.1 broadcast_in_dim.52
  1.1 1.6 %gather_fusion = s32[5,512]{1,0:T(8,128)S(1)} fusion(s32[31,512]{1,0:T(8,128)} %param.5, s32[1024]{0:T(1024)S(1)} %pad_clamp_fusion), kind=kCustom, calls=%fused_computation | custom fusion | bytes 20500 | tf_op jit(solution)/shard_map/jit(_take)/gather | solution.py:457
  2.8 0.1 broadcast_select_fusion.pivot_ref
  2.8 0.1 gather.12
  2.9 0.1 select_subtract_fusion
  3.0 0.6 fusion
  3.6 1.4 convert_reduce_fusion
  5.0 1.4 select_reduce_fusion
  6.5 0.1 reduce_sum.23
  6.5 0.1 sub.43
  6.6 0.1 sub.44
  6.7 0.1 add.78
  6.8 0.1 add.79
  6.9 0.6 pad_add_fusion.index_ref
  7.5 0.0 copy-done
  7.5 6.9 %fusion.4 = f32[1024,1024]{1,0:T(8,128)} fusion(bf16[1536,1024]{1,0:T(8,128)(2,1)S(1)} %copy-done, bf16[1024,1536]{1,0:T(8,128)(2,1)} %param.3), kind=kOutput, calls=%fused_computation.21 | convolution fusion | flops 3221225472 | bytes 10485760 | tf_op jit(solution)/shard_map/dot_general | solution.py:472
  14.5 60.4 %shard_map.50 = (f32[16,8,64,128]{3,2,1,0:T(8,128)}, f32[64,512]{1,0:T(8,128)}) custom-call(f32[4,4,64,1024]{3,2,1,0:T(8,128)} %bitcast.19, s32[20,1,256]{2,1,0:T(1,128)} %pad_add_fusion.index_ref), custom_call_target="tpu_custom_call" | custom-call | tf_op jit(solution)/shard_map/pallas_call | solution.py:268
  74.9 0.0 copy-start.2
  74.9 4.1 %shard_map.51.u_ref = f32[512,512]{1,0:T(8,128)} custom-call(f32[16,8,64,128]{3,2,1,0:T(8,128)} %get-tuple-element.4.z_ref), custom_call_target="tpu_custom_call" | custom-call | tf_op jit(solution)/shard_map/pallas_call | solution.py:444
  79.1 0.0 copy-start.1
  79.1 1.2 copy-done.1
  80.3 66.7 %shard_map.52 = f32[5,64,512]{2,1,0:T(8,128)S(1)} custom-call(f32[512,512]{1,0:T(8,128)S(1)} %copy-done.1, s32[5,1,512]{2,1,0:T(1,128)S(1)} %broadcast_select_fusion.pivot_ref, s32[5,1,32]{2,1,0:T(1,128)S(1)} %constant_dynamic-slice_fusion.other_ref), custom_call_target="tpu_custom_call" | custom-call | tf_op jit(solution)/shard_map/pallas_call | solution.py:345
  146.9 0.8 copy.15
  147.8 0.0 copy-done.2
  147.8 0.7 copy.16
  (10 shorter events, 0.1 us)
Async XLA Ops:
  0.6 6.9 %copy-start = (bf16[1536,1024]{1,0:T(8,128)(2,1)S(1)}, bf16[1536,1024]{1,0:T(8,128)(2,1)}, u32[]{:S(2)}) copy-start(bf16[1536,1024]{1,0:T(8,128)(2,1)} %param.4) | copy-start | bytes 9437188
  74.9 72.9 %copy-start.2 = (f32[64,512]{1,0:T(8,128)S(1)}, f32[64,512]{1,0:T(8,128)}, u32[]{:S(2)}) copy-start(f32[64,512]{1,0:T(8,128)} %get-tuple-element.17) | copy-start | bytes 393220
  79.1 1.2 copy-start.1

commit v3 on v0

v3 whole, which is shorter than its diff:
```python
import jax
import jax.numpy as jnp
from jax import lax
from jax.experimental import pallas as pl
from jax.experimental.pallas import tpu as pltpu
from jax.sharding import PartitionSpec as P

HI = lax.Precision.HIGHEST
MESH = pl.DeviceIdType.MESH
SOLVERS = (
    (0, 0, 0, 0), (0, 0, 1, 10), (0, 1, 0, 2), (0, 1, 1, 8), (1, 0, 0, 5), (1, 0, 1, 15),
    (2, 1, 0, 7), (2, 1, 1, 13), (3, 0, 0, 3), (3, 0, 1, 9), (4, 1, 0, 6), (4, 1, 1, 12),
)


def bit(value, place):
    return lax.rem(value // (1 << place), 2)


def flip(value, mask):
    for place in range(4):
        if mask >> place & 1:
            value = value + (1 << place) * (1 - 2 * bit(value, place))
    return value


def send(src, dst, send_sem, recv_sem, device):
    return pltpu.make_async_remote_copy(
        src_ref=src, dst_ref=dst, send_sem=send_sem, recv_sem=recv_sem, device_id=device, device_id_type=MESH
    )


def row_of(table, node):
    rows = lax.broadcasted_iota(jnp.int32, table.shape, 0)
    return jnp.sum(jnp.where(rows == node, table, 0), axis=0, keepdims=True)


def split3(value):
    high = value.astype(jnp.bfloat16)
    rest = value - high.astype(jnp.float32)
    middle = rest.astype(jnp.bfloat16)
    low = (rest - middle.astype(jnp.float32)).astype(jnp.bfloat16)
    return jnp.concatenate([high, middle, low], axis=0)


def permuted(src, order):
    rows = src.shape[0]
    out = jnp.dot(split3(src), order, preferred_element_type=jnp.float32)
    return (out[:rows] + out[rows : 2 * rows]) + out[2 * rows :]


def one_hot_order(pivots, start):
    src = lax.broadcasted_iota(jnp.int32, (256, 128), 0)
    lane = lax.broadcasted_iota(jnp.int32, (256, 128), 1)
    chosen = jnp.where(src == pivots - start, 1.0, 0.0)
    ones = jnp.full((128, 128), 1.0, jnp.bfloat16)
    free = 1.0 - jnp.dot(chosen.astype(jnp.bfloat16), ones, preferred_element_type=jnp.float32)
    row = lax.broadcasted_iota(jnp.int32, (256, 256), 0)
    column = lax.broadcasted_iota(jnp.int32, (256, 256), 1)
    before = jnp.where(jnp.logical_and(column < row, column // 64 == row // 64), 1.0, 0.0).astype(jnp.bfloat16)
    rank = jnp.dot(before, free.astype(jnp.bfloat16), preferred_element_type=jnp.float32)
    place = rank + (32 * (src // 64)).astype(jnp.float32)
    rest = jnp.where(jnp.logical_and(free > 0.5, place == lane.astype(jnp.float32)), 1.0, 0.0)
    return chosen.astype(jnp.bfloat16), rest.astype(jnp.bfloat16)


def gather_kernel(
    front_any, sample_any, pivot_ref, z_ref, top_ref,
    front_ref, sample_ref, turned_ref, p_ref,
    hop1, comb1, near1, sum1, hop2, comb2, near2, order_ref, y_ref,
    a1_ref, a2_ref, a3_ref, r1_ref, r2_ref, r3_ref, r4_ref,
    load_sem, rs_send, rs_recv, leaf_send, leaf_recv, z_send, z_recv, z_local,
):
    leaf, grp = lax.axis_index("leaf"), lax.axis_index("grp")
    y, x = grp // 4, lax.rem(grp, 4)
    core = lax.rem(leaf, 2)
    base = leaf - core

    loads = [
        pltpu.make_async_copy(sample_any, sample_ref, load_sem.at[0]),
        pltpu.make_async_copy(front_any, front_ref, load_sem.at[1]),
    ]
    for load in loads:
        load.start()
    barrier = pltpu.get_barrier_semaphore()
    for other in range(1, 16):
        pl.semaphore_signal(barrier, inc=1, device_id=(leaf, lax.rem(grp + other, 16)), device_id_type=MESH)
        pl.semaphore_signal(barrier, inc=1, device_id=(lax.rem(leaf + other, 16), grp), device_id_type=MESH)

    started = []

    def begin(copy):
        copy.start()
        started.append(copy)
        return copy

    def neighbour(along_x, offset):
        if along_x:
            return (leaf, y * 4 + lax.rem(x + offset, 4))
        return (leaf, lax.rem(y + offset, 4) * 4 + x)

    def source(phase, stream, chunk, sub):
        half = stream % 2
        if phase == 0:
            lanes = pl.ds(512 * half + 256 * (stream // 2), 256)
            if half == 0:
                return p_ref.at[pl.ds(2 * sub, 2), chunk, :, lanes]
            return p_ref.at[chunk, pl.ds(2 * sub, 2), :, lanes]
        return sum1.at[stream, chunk, pl.ds(32 * sub, 32), :]

    def landing(phase, stream, way, sub):
        if phase == 0:
            return near1.at[stream, way, pl.ds(2 * sub, 2), :, :]
        return near2.at[stream, way, pl.ds(32 * sub, 32), :]

    hops, combs = (hop1, hop2), (comb1, comb2)
    rings = {}

    def ring(phase, stream, way, kind, src, dst):
        along_x = (phase == 0) == (stream % 2 == 0)
        to = neighbour(along_x, 1 if way == 0 else 3)
        rings[phase, stream, way, kind] = begin(
            send(src, dst, rs_send.at[phase, stream, way, kind], rs_recv.at[phase, stream, way, kind], to)
        )

    def position(phase, stream):
        return x if (phase == 0) == (stream % 2 == 0) else y

    def ring_hop(phase, stream):
        at = position(phase, stream)
        for way in range(2):
            ring(phase, stream, way, 0, source(phase, stream, lax.rem(at + 2, 4), way), hops[phase].at[stream, way])

    def ring_own(phase, stream):
        at = position(phase, stream)
        for way in range(2):
            chunk = lax.rem(at + (1 if way == 0 else 3), 4)
            ring(phase, stream, way, 1, source(phase, stream, chunk, 1 - way), landing(phase, stream, way, 1 - way))

    def ring_join(phase, stream):
        at = position(phase, stream)
        for way in range(2):
            chunk = lax.rem(at + (1 if way == 0 else 3), 4)
            rings[phase, stream, way, 0].wait_recv()
            combs[phase][stream, way] = hops[phase][stream, way] + source(phase, stream, chunk, way)[...]
            ring(phase, stream, way, 2, combs[phase].at[stream, way], landing(phase, stream, way, way))

    def ring_last(phase, stream):
        for way in range(2):
            for kind in (1, 2):
                rings[phase, stream, way, kind].wait_recv()
        half = stream % 2
        if phase == 0:
            lanes = pl.ds(512 * half + 256 * (stream // 2), 256)
            own = p_ref[:, x, :, lanes] if half == 0 else p_ref[y, :, :, lanes]
            sum1[stream] = (near1[stream, 0] + own) + near1[stream, 1]
            return None
        own = sum1[stream, position(1, stream)]
        return (near2[stream, 0] + own) + near2[stream, 1]

    loads[0].wait()
    for c in range(8):
        turned_ref[128 * c : 128 * c + 128, :] = sample_ref[:, 128 * c : 128 * c + 128].T
    loads[1].wait()
    for stream in range(4):
        low = 512 * (stream % 2) + 256 * (stream // 2)
        for c in range(4):
            product = lax.dot_general(
                turned_ref[256 * c : 256 * c + 256, :], front_ref[low : low + 256, :], (((1,), (1,)), ((), ())),
                preferred_element_type=jnp.float32,
            )
            for b in range(4):
                p_ref[c, b, :, low : low + 256] = product[64 * b : 64 * b + 64]
        if stream == 0:
            pl.semaphore_wait(barrier, 30)
        ring_hop(0, stream)
        if stream < 2:
            ring_own(0, stream)

    def orders(level, block):
        node = 32 - (32 >> level) + leaf // (1 << level)
        chosen, rest = one_hot_order(row_of(pivot_ref[:, 128 * block : 128 * block + 128], node), 256 * block)
        order_ref[4 * level + block, :, 0:128] = chosen
        order_ref[4 * level + block, :, 128:256] = rest

    for block in range(4):
        orders(0, block)
        orders(1, block)
    ring_join(0, 0)
    ring_join(0, 1)
    ring_own(0, 2)
    ring_own(0, 3)
    for block in range(4):
        orders(2, block)
        orders(3, block)
        orders(4, block)
    for stream in (0, 1):
        ring_last(0, stream)
        ring_hop(1, stream)
        ring_own(1, stream)
    ring_join(0, 2)
    ring_join(0, 3)
    ring_join(1, 0)
    ring_join(1, 1)
    for stream in (2, 3):
        ring_last(0, stream)
        ring_hop(1, stream)
        ring_own(1, stream)

    def select(level, block, value):
        chosen = permuted(value, order_ref[4 * level + block])
        y_ref[level, 2 + block] = chosen[:, :128]
        y_ref[level, block + 4 * (block // 2)] = chosen[:, 128:]

    select(0, 0, ring_last(1, 0))
    select(0, 2, ring_last(1, 1))
    ring_join(1, 2)
    ring_join(1, 3)
    select(0, 1, ring_last(1, 2))
    select(0, 3, ring_last(1, 3))

    def each_solver(level, remote, local):
        for number, (of_level, of_core, half, place) in enumerate(SOLVERS):
            if of_level != level:
                continue
            src = y_ref.at[level, pl.ds(2 * half, 6)]

            def to(slot, target):
                return send(src, z_ref.at[slot], z_send.at[number], z_recv.at[slot], (leaf, target))

            @pl.when(jnp.logical_and(core == of_core, grp != place))
            def _():
                remote(to(grp, place))

            @pl.when(jnp.logical_and(core == of_core, grp == place))
            def _():
                local(pltpu.make_async_copy(src, z_ref.at[grp], z_local), to, place)

    def to_solver(level):
        each_solver(level, lambda copy: copy.start(), lambda copy, to, place: copy.start())

    def solver_end(level):
        def collect(copy, to, place):
            copy.wait()
            for source_grp in range(16):
                if source_grp != place:
                    to(source_grp, source_grp).wait_recv()

        each_solver(level, lambda copy: copy.wait_send(), collect)

    def both(first, second):
        return jnp.concatenate([first, second], axis=1)

    up = send(y_ref.at[0, pl.ds(2, 4)], r1_ref, leaf_send.at[0], leaf_recv.at[0], (base, grp))

    @pl.when(core == 1)
    def _():
        up.start()

    def chosen_only(level, block, value):
        return permuted(value, order_ref[4 * level + block][:, :128])

    kept = []

    def share(number, src, dst_ref, slot, recv, to_core, masks, value):
        for n, mask in enumerate(masks):
            copy = send(
                src, dst_ref.at[slot], leaf_send.at[number + n], leaf_recv.at[recv + slot], (flip(base, mask) + to_core, grp)
            )
            if mask == 0:

                @pl.when(core != to_core)
                def _():
                    copy.start()

                @pl.when(core == to_core)
                def _():
                    dst_ref[slot] = value

                kept.append((copy, to_core))
            else:
                begin(copy)

    for i in range(2):
        a1_ref[i] = chosen_only(1, 2 * core + i, both(y_ref[0, 2 + 2 * i], y_ref[0, 3 + 2 * i]))
    part1 = a1_ref[...]
    share(1, a1_ref, r2_ref, lax.rem(leaf, 4), 1, 1, (2, 0), part1)
    part2 = chosen_only(2, lax.rem(leaf, 4), both(part1[0], part1[1]))
    a2_ref[...] = part2
    share(3, a2_ref, r3_ref, lax.rem(leaf, 8), 5, 0, (4, 6, 2, 0), part2)
    zero = jnp.zeros_like(part2)
    spread_out = both(jnp.where(core == 0, part2, zero), jnp.where(core == 0, zero, part2))
    placed = chosen_only(3, lax.rem(leaf, 8) // 2, spread_out)
    part3 = placed[:32] + pltpu.roll(placed[32:], 64, 1)
    a3_ref[...] = part3
    share(7, a3_ref, r4_ref, leaf, 13, 1, (8, 10, 6, 12, 14, 4, 2, 0), part3)
    to_solver(0)

    def arrived(ref, recv, slot):
        @pl.when(slot != lax.rem(leaf, ref.shape[0]))
        def _():
            send(ref.at[slot], ref.at[slot], leaf_send.at[0], leaf_recv.at[recv + slot], (base + 1 - core, grp)).wait_recv()

    @pl.when(core == 0)
    def _():
        for i in range(2):
            select(1, i, both(y_ref[0, 2 + 2 * i], y_ref[0, 3 + 2 * i]))
        send(r1_ref, r1_ref, leaf_send.at[0], leaf_recv.at[0], (base + 1, grp)).wait_recv()
        for i in range(2):
            select(1, 2 + i, both(r1_ref[2 * i], r1_ref[2 * i + 1]))

    to_solver(1)

    @pl.when(core == 1)
    def _():
        for s in range(4):
            arrived(r2_ref, 1, s)
            select(2, s, both(r2_ref[s, 0], r2_ref[s, 1]))

    to_solver(2)

    @pl.when(core == 0)
    def _():
        for s in range(4):
            arrived(r3_ref, 5, 2 * s)
            arrived(r3_ref, 5, 2 * s + 1)
            select(3, s, both(r3_ref[2 * s], r3_ref[2 * s + 1]))

    to_solver(3)

    @pl.when(core == 1)
    def _():
        low_lanes = lax.broadcasted_iota(jnp.int32, (32, 128), 1) < 64
        for s in range(16):
            arrived(r4_ref, 13, s)
        joined = []
        for i in range(8):
            even, odd = r4_ref[2 * i], r4_ref[2 * i + 1]
            upper = jnp.where(low_lanes, even, odd)
            lower = pltpu.roll(jnp.where(low_lanes, odd, even), 64, 1)
            joined.append(jnp.concatenate([upper, lower], axis=0))
        for s in range(4):
            select(4, s, both(joined[2 * s], joined[2 * s + 1]))

    to_solver(4)

    top = send(y_ref.at[4, pl.ds(2, 4)], y_ref.at[4, pl.ds(2, 4)], leaf_send.at[15], leaf_recv.at[29], (base, grp))

    @pl.when(core == 1)
    def _():
        top.start()
        up.wait_send()
        top.wait_send()

    @pl.when(core == 0)
    def _():
        top.wait_recv()

    for b in range(4):
        top_ref[:, 128 * b : 128 * b + 128] = y_ref[4, 2 + b]

    for copy, to_core in kept:

        @pl.when(core != to_core)
        def _():
            copy.wait_send()

    for copy in started:
        copy.wait_send()
    for level in range(5):
        solver_end(level)


def gathered(front_rows, sample_matrix, pivots):
    dma = pltpu.SemaphoreType.DMA
    f32 = lambda *shape: pltpu.VMEM(shape, jnp.float32)
    bf16 = lambda *shape: pltpu.VMEM(shape, jnp.bfloat16)
    anywhere = pl.BlockSpec(memory_space=pl.ANY)
    vmem = pl.BlockSpec(memory_space=pltpu.VMEM)
    return pl.pallas_call(
        gather_kernel,
        out_shape=(jax.ShapeDtypeStruct((16, 6, 64, 128), jnp.float32), jax.ShapeDtypeStruct((64, 512), jnp.float32)),
        in_specs=[anywhere, anywhere, vmem],
        out_specs=(anywhere, vmem),
        scratch_shapes=[
            bf16(1024, 1536), bf16(1536, 1024), bf16(1024, 1536), f32(4, 4, 64, 1024),
            f32(4, 2, 2, 64, 256), f32(4, 2, 2, 64, 256), f32(4, 2, 4, 64, 256), f32(4, 4, 64, 256),
            f32(4, 2, 32, 256), f32(4, 2, 32, 256), f32(4, 2, 64, 256), bf16(20, 256, 256), f32(5, 8, 64, 128),
            f32(2, 64, 128), f32(64, 128), f32(32, 128), f32(4, 64, 128), f32(4, 2, 64, 128), f32(8, 64, 128), f32(16, 32, 128),
            dma((2,)), dma((2, 4, 2, 3)), dma((2, 4, 2, 3)), dma((16,)), dma((30,)), dma((12,)), dma((16,)), dma,
        ],
        compiler_params=pltpu.CompilerParams(collective_id=1, has_side_effects=True, vmem_limit_bytes=56 * 1024 * 1024),
    )(front_rows, sample_matrix, pivots)


def solver_role():
    grp, core = lax.axis_index("grp"), lax.rem(lax.axis_index("leaf"), 2)
    active, half = 0, 0
    for _, of_core, of_half, place in SOLVERS:
        here = jnp.where(jnp.logical_and(core == of_core, grp == place), 1, 0)
        active, half = active + here, half + of_half * here
    return active > 0, half


def spread_kernel(u_ref, pivot_ref, out_ref, rows_ref, u_send, u_recv, u_local):
    leaf, grp = lax.axis_index("leaf"), lax.axis_index("grp")
    core = lax.rem(leaf, 2)
    base = leaf - core
    barrier = pltpu.get_barrier_semaphore()
    for other in range(1, 16):
        pl.semaphore_signal(barrier, inc=1, device_id=(leaf, lax.rem(grp + other, 16)), device_id_type=MESH)
    for other in range(16):
        pl.semaphore_signal(barrier, inc=1, device_id=(base + 1 - core, other), device_id_type=MESH)
    pl.semaphore_wait(barrier, 31)

    def each(level, of_core, half, place, act):
        def to(target_core, target, slot):
            return send(
                u_ref.at[pl.ds(32 * (target - 8 * half), 32)], rows_ref.at[level], u_send.at[slot], u_recv.at[level],
                (base + target_core, target),
            )

        @pl.when(jnp.logical_and(core == of_core, grp == place))
        def _():
            for target in range(8 * half, 8 * half + 8):
                if target != place:
                    act(to(of_core, target, target))
                if level > 0:
                    act(to(1 - of_core, target, 16 + target))

    for solver in SOLVERS:
        each(*solver, lambda copy: copy.start())

    before = jnp.where(
        lax.broadcasted_iota(jnp.int32, (64, 64), 1) < lax.broadcasted_iota(jnp.int32, (64, 64), 0), 1.0, 0.0
    ).astype(jnp.bfloat16)
    ones = jnp.full((512, 128), 1.0, jnp.bfloat16)
    spots = []
    for level in range(5):
        node = 32 - (32 >> level) + leaf // (1 << level)
        at = grp * 64 + lax.broadcasted_iota(jnp.int32, (64, 512), 0)
        is_pivot = jnp.where(at == row_of(pivot_ref[...], node), 1.0, 0.0)
        out_ref[level] = is_pivot
        free = 1.0 - jnp.dot(is_pivot.astype(jnp.bfloat16), ones, preferred_element_type=jnp.float32)
        rank = jnp.dot(before, free.astype(jnp.bfloat16), preferred_element_type=jnp.float32)
        slot = lax.broadcasted_iota(jnp.int32, (64, 128), 1).astype(jnp.float32)
        spots.append(jnp.where(jnp.logical_and(free > 0.5, rank == slot), 1.0, 0.0)[:, :32])

    for level, of_core, half, place in SOLVERS:
        own = jnp.logical_and(core == of_core, grp == place)
        if place // 8 == half:

            @pl.when(own)
            def _():
                copy = pltpu.make_async_copy(u_ref.at[pl.ds(32 * (place - 8 * half), 32)], rows_ref.at[level], u_local)
                copy.start()
                copy.wait()

            gets = jnp.logical_and(grp // 8 == half, jnp.logical_not(own))
        else:
            gets = grp // 8 == half
        if level == 0:
            gets = jnp.logical_and(core == of_core, gets)

        @pl.when(gets)
        def _():
            send(
                u_ref.at[pl.ds(0, 32)], rows_ref.at[level], u_send.at[0], u_recv.at[level], (base + 1 - core, grp)
            ).wait_recv()

    for level in range(5):
        out_ref[level] += lax.dot_general(
            spots[level], rows_ref[level], (((1,), (0,)), ((), ())), precision=HI, preferred_element_type=jnp.float32
        )
    for solver in SOLVERS:
        each(*solver, lambda copy: copy.wait_send())


def spread(u, pivots):
    dma = pltpu.SemaphoreType.DMA
    return pl.pallas_call(
        spread_kernel,
        out_shape=jax.ShapeDtypeStruct((5, 64, 512), jnp.float32),
        in_specs=[pl.BlockSpec(memory_space=pltpu.VMEM)] * 2,
        out_specs=pl.BlockSpec(memory_space=pltpu.VMEM),
        scratch_shapes=[pltpu.VMEM((5, 32, 512), jnp.float32), dma((32,)), dma((5,)), dma],
        compiler_params=pltpu.CompilerParams(collective_id=2, has_side_effects=True, vmem_limit_bytes=16 * 1024 * 1024),
    )(u, pivots)


def wide(value):
    return jnp.broadcast_to(value, (8, 128))


def small_inverse(columns, sub):
    columns = list(columns)
    for k in range(8):
        rows = [wide(column[k : k + 1, :]) for column in columns]
        scale = 1.0 / rows[k]
        here = sub == k
        lead = columns[k]
        for j in range(8):
            if j != k:
                row = rows[j] * scale
                columns[j] = jnp.where(here, row, columns[j] - lead * row)
        columns[k] = jnp.where(here, scale, -(lead * scale))
    return columns


def weighted(columns, rows):
    even, odd = columns[0] * rows[0], columns[1] * rows[1]
    for j in range(2, 8, 2):
        even = even + columns[j] * rows[j]
        odd = odd + columns[j + 1] * rows[j + 1]
    return even + odd


def invert(read):
    lane = lax.broadcasted_iota(jnp.int32, (8, 128), 1)
    sub = lax.broadcasted_iota(jnp.int32, (8, 128), 0)
    eye = jnp.where(lane == sub, 1.0, 0.0)

    def eight(_, blocks):
        corner = small_inverse([wide(blocks[0][:, 8 + j : 9 + j]) for j in range(8)], sub)
        columns = [[wide(block[:, 8 + j : 9 + j]) for j in range(8)] for block in blocks[1:]]
        rolled = [pltpu.roll(block, 120, 1) for block in blocks]
        top = jnp.where(lane < 8, eye, rolled[0])
        new = weighted(corner, [wide(top[j : j + 1]) for j in range(8)])
        rows = [wide(new[j : j + 1]) for j in range(8)]
        rest = [jnp.where(lane < 8, 0.0, block) - weighted(cols, rows) for cols, block in zip(columns, rolled[1:])]
        return tuple(rest + [new])

    blocks = lax.fori_loop(0, 16, eight, tuple(pltpu.roll(read(i), 8, 1) for i in range(16)))
    return jnp.concatenate([pltpu.roll(block, 120, 1) for block in blocks], axis=0)


def dot(a, b):
    return lax.dot_general(a, b, (((1,), (0,)), ((), ())), precision=HI, preferred_element_type=jnp.float32)


def solve_kernel(z_ref, u_ref, m_ref):
    step = pl.program_id(0)
    active, half = solver_role()

    @pl.when(step == 0)
    def _():
        m_ref[...] = jnp.zeros_like(m_ref)

    @pl.when(active)
    def _():
        rows = []
        for g in range(4):
            skeleton = [z_ref[g, 2 - 2 * half + b] for b in range(4)]
            rows.append(jnp.concatenate(skeleton + [z_ref[g, 4 * half + b] for b in range(2)], axis=1))
        z = jnp.concatenate(rows, axis=0)
        m_ref[...] += lax.dot_general(
            z, z[:, :512], (((0,), (0,)), ((), ())), precision=HI, preferred_element_type=jnp.float32
        )

    @pl.when(jnp.logical_and(active, step == 3))
    def _():
        for p in range(4):
            at = 128 * p
            dinv = invert(lambda i: m_ref[at + 8 * i : at + 8 * i + 8, at : at + 128])
            lead = m_ref[at : at + 128, :]
            for low in range(at + 128, 768, 128):
                w = dot(m_ref[low : low + 128, at : at + 128], dinv)
                for q in range(4):
                    if q != p:
                        m_ref[low : low + 128, 128 * q : 128 * q + 128] -= dot(w, lead[:, 128 * q : 128 * q + 128])
                m_ref[low : low + 128, at : at + 128] = w
        u_ref[...] = m_ref[512:, :]


def solve(z):
    return pl.pallas_call(
        solve_kernel,
        grid=(4,),
        in_specs=[pl.BlockSpec((4, 6, 64, 128), lambda i: (i, 0, 0, 0))],
        out_specs=pl.BlockSpec((256, 512), lambda i: (0, 0)),
        out_shape=jax.ShapeDtypeStruct((256, 512), jnp.float32),
        scratch_shapes=[pltpu.VMEM((768, 512), jnp.float32)],
        compiler_params=pltpu.CompilerParams(dimension_semantics=("arbitrary",), vmem_limit_bytes=56 * 1024 * 1024),
    )(z)


def on_device(front_rows, sample_matrix, pivots):
    z, top = gathered(front_rows, sample_matrix, pivots)
    bases = spread(solve(z), pivots)
    return (bases[:, None], top)


def solution(mesh):
    return jax.shard_map(
        on_device,
        mesh=mesh,
        in_specs=(P("leaf", "grp"), P("grp", None), P()),
        out_specs=(P(None, "leaf", "grp", None), P("grp", None)),
        check_vma=False,
    )
```

time: 1070 us -> 119 us (0.11)
  the two profiles are of different devices: /device:TPU:30 before, /device:TPU:8 now
where the time goes in v3:
time: 119 us
  Pallas kernels  115 us (97%)
  local copies, waits for them, and re-layouts  2.55 us (2%)
    pallas_call x1, Pallas kernels, gathered(): pl.pallas_call(gather_kernel, out_shape=(jax.ShapeDtypeStruct((16, 6, 64,...  64.6 us
    pallas_call x1, Pallas kernels, spread(): pl.pallas_call(spread_kernel, out_shape=jax.ShapeDtypeStruct((5, 64, 512)...  47.4 us
    pallas_call x1, Pallas kernels, solve(): pl.pallas_call(solve_kernel, grid=(4,), in_specs=[pl.BlockSpec((4, 6, 64,...  3.51 us
    unnamed x8, local copies, waits for them, and re-layouts  2.55 us

profile of v3, /device:TPU:8, one launch (start us, length us, event | category | flops | bytes accessed | tf_op | source)
XLA Modules:
  0.0 118.7 jit_solution(5500826160167731902)
XLA Ops:
  0.6 64.6 %shard_map.50 = (f32[16,6,64,128]{3,2,1,0:T(8,128)}, f32[64,512]{1,0:T(8,128)}) custom-call(bf16[1024,1536]{1,0:T(8,128)(2,1)} %front_any.1, bf16[1536,1024]{1,0:T(8,128)(2,1)} %sample_any.1, s32[31,512]{1,0:T(8,128)} %pivot_ref.3), custom_call_target="tpu_custom_call" | custom-call | tf_op jit(solution)/shard_map/pallas_call | solution.py:380
  65.2 0.0 copy-start.1
  65.3 0.0 copy-start.2
  65.3 3.5 %shard_map.51.u_ref = f32[256,512]{1,0:T(8,128)} custom-call(f32[16,6,64,128]{3,2,1,0:T(8,128)} %get-tuple-element.4.z_ref), custom_call_target="tpu_custom_call" | custom-call | tf_op jit(solution)/shard_map/pallas_call | solution.py:576
  68.8 0.0 copy-done.1
  68.8 0.0 copy-start
  68.8 1.0 copy-done
  69.8 47.4 %shard_map.52 = f32[5,64,512]{2,1,0:T(8,128)S(1)} custom-call(f32[256,512]{1,0:T(8,128)S(1)} %copy-done, s32[31,512]{1,0:T(8,128)S(1)} %copy-done.1), custom_call_target="tpu_custom_call" | custom-call | tf_op jit(solution)/shard_map/pallas_call | solution.py:481
  117.2 0.8 copy.8
  118.0 0.0 copy-done.2
  118.0 0.7 copy.9
Async XLA Ops:
  65.2 3.5 %copy-start.1 = (s32[31,512]{1,0:T(8,128)S(1)}, s32[31,512]{1,0:T(8,128)}, u32[]{:S(2)}) copy-start(s32[31,512]{1,0:T(8,128)} %pivot_ref.3) | copy-start | bytes 190468
  65.3 52.8 %copy-start.2 = (f32[64,512]{1,0:T(8,128)S(1)}, f32[64,512]{1,0:T(8,128)}, u32[]{:S(2)}) copy-start(f32[64,512]{1,0:T(8,128)} %get-tuple-element.11) | copy-start | bytes 393220
  68.8 1.0 copy-start

commit v4 on v3

--- a/solution.py
+++ b/solution.py
@@ -7,10 +7,54 @@
 
 HI = lax.Precision.HIGHEST
 MESH = pl.DeviceIdType.MESH
-SOLVERS = (
-    (0, 0, 0, 0), (0, 0, 1, 10), (0, 1, 0, 2), (0, 1, 1, 8), (1, 0, 0, 5), (1, 0, 1, 15),
-    (2, 1, 0, 7), (2, 1, 1, 13), (3, 0, 0, 3), (3, 0, 1, 9), (4, 1, 0, 6), (4, 1, 1, 12),
+ROOTS = ((8, 7, 5), (2, 10, 13))
+LEVELS = ((0, 1, 3), (0, 2, 4))
+FIRST = (
+    ((4, 4, 12, 12, 8, 8, 11, 8, 8, 8, 9, 8, 8, 9, 11, 12), (1, 2, 2, 2, 3, 6, 2, 6, 1, 14, 6, 14, 3, 2, 2, 2)),
+    ((7, 4, 6, 7, 7, 6, 7, 7, 11, 4, 7, 7, 3, 3, 7, 11), (6, 14, 6, 14, 11, 9, 10, 10, 9, 10, 10, 10, 9, 10, 10, 11)),
+    ((5, 5, 5, 4, 5, 5, 5, 6, 9, 5, 9, 6, 1, 9, 1, 4), (13, 13, 13, 12, 1, 1, 9, 9, 13, 13, 14, 12, 13, 13, 13, 14)),
 )
+SLOT = (
+    ((0, 1, 0, 1, 0, 0, 0, 0, 0, 0, 0, 0, 0, 1, 1, 2), (0, 0, 0, 0, 0, 0, 0, 1, 1, 0, 2, 1, 1, 0, 0, 0)),
+    ((0, 0, 0, 0, 0, 1, 0, 0, 0, 1, 0, 0, 0, 1, 0, 1), (0, 0, 1, 1, 0, 0, 0, 0, 1, 0, 0, 0, 2, 0, 0, 1)),
+    ((0, 0, 0, 0, 0, 0, 0, 0, 0, 0, 1, 1, 0, 2, 1, 1), (0, 0, 0, 0, 0, 1, 0, 1, 0, 0, 0, 1, 0, 0, 0, 1)),
+)
+PASS_ON = (
+    (
+        ((0, 0, 0, 0, 1, 0, 0, 0, 0, 11, 0, 7, 3, 0, 0, 0), (0, 1, 0, 5, 0, 0, 6, 0, 0, 0, 0, 0, 0, 0, 10, 0)),
+        ((0, 0, 0, 0, 2, 0, 0, 0, 0, 14, 0, 15, 4, 0, 0, 0), (0, 9, 0, 13, 0, 0, 8, 0, 0, 0, 0, 0, 0, 0, 12, 0)),
+        ((0, 0, 0, 0, 0, 0, 0, 0, 0, 0, 0, 0, 16, 0, 0, 0), (0, 0, 0, 0, 0, 0, 11, 0, 0, 0, 0, 0, 0, 0, 0, 0)),
+    ),
+    (
+        ((0, 0, 0, 13, 2, 0, 3, 0, 0, 0, 0, 9, 0, 0, 0, 0), (0, 0, 0, 0, 0, 0, 1, 0, 0, 6, 0, 5, 0, 0, 2, 0)),
+        ((0, 0, 0, 14, 10, 0, 6, 0, 0, 0, 0, 16, 0, 0, 0, 0), (0, 0, 0, 0, 0, 0, 3, 0, 0, 9, 0, 16, 0, 0, 4, 0)),
+        ((0, 0, 0, 0, 0, 0, 0, 0, 0, 0, 0, 0, 0, 0, 0, 0), (0, 0, 0, 0, 0, 0, 0, 0, 0, 13, 0, 0, 0, 0, 0, 0)),
+    ),
+    (
+        ((0, 13, 0, 0, 4, 0, 8, 0, 0, 9, 0, 0, 0, 0, 0, 0), (0, 5, 0, 0, 0, 0, 0, 0, 0, 7, 0, 0, 4, 0, 11, 0)),
+        ((0, 15, 0, 0, 16, 0, 12, 0, 0, 11, 0, 0, 0, 0, 0, 0), (0, 6, 0, 0, 0, 0, 0, 0, 0, 8, 0, 0, 12, 0, 16, 0)),
+        ((0, 0, 0, 0, 0, 0, 0, 0, 0, 14, 0, 0, 0, 0, 0, 0), (0, 0, 0, 0, 0, 0, 0, 0, 0, 0, 0, 0, 0, 0, 0, 0)),
+    ),
+)
+
+
+def lookup(table, core, grp):
+    at, value = 16 * core + grp, 0
+    for position, entry in enumerate(table[0] + table[1]):
+        if entry:
+            value = value + jnp.where(at == position, entry, 0)
+    return value
+
+
+def roles():
+    grp, core = lax.axis_index("grp"), lax.rem(lax.axis_index("leaf"), 2)
+    main, twin = 0, 0
+    for of_core in range(2):
+        for root in ROOTS[of_core]:
+            here = jnp.where(grp == root, 1, 0)
+            main = main + here * jnp.where(core == of_core, 1, 0)
+            twin = twin + here * jnp.where(core == of_core, 0, 1)
+    return main, twin
 
 
 def bit(value, place):
@@ -65,11 +109,12 @@
 
 
 def gather_kernel(
-    front_any, sample_any, pivot_ref, z_ref, top_ref,
+    front_any, sample_any, pivot_ref, out_ref, top_ref,
     front_ref, sample_ref, turned_ref, p_ref,
     hop1, comb1, near1, sum1, hop2, comb2, near2, order_ref, y_ref,
-    a1_ref, a2_ref, a3_ref, r1_ref, r2_ref, r3_ref, r4_ref,
-    load_sem, rs_send, rs_recv, leaf_send, leaf_recv, z_send, z_recv, z_local,
+    a1_ref, a2_ref, a3_ref, r1_ref, r2_ref, r3_ref, r4_ref, rt_ref, relay_ref, z_ref, m_ref, spot_ref, rows_ref,
+    load_sem, rs_send, rs_recv, leaf_send, leaf_recv, y_send, relay_send, relay_recv, z_recv, z_local, twin_send, twin_recv,
+    u_send, u_recv, u_onward,
 ):
     leaf, grp = lax.axis_index("leaf"), lax.axis_index("grp")
     y, x = grp // 4, lax.rem(grp, 4)
@@ -209,8 +254,9 @@
 
     def select(level, block, value):
         chosen = permuted(value, order_ref[4 * level + block])
-        y_ref[level, 2 + block] = chosen[:, :128]
-        y_ref[level, block + 4 * (block // 2)] = chosen[:, 128:]
+        task = (level + 1) // 2
+        y_ref[task, 2 + block] = chosen[:, :128]
+        y_ref[task, block + 4 * (block // 2)] = chosen[:, 128:]
 
     select(0, 0, ring_last(1, 0))
     select(0, 2, ring_last(1, 1))
@@ -219,38 +265,52 @@
     select(0, 1, ring_last(1, 2))
     select(0, 3, ring_last(1, 3))
 
-    def each_solver(level, remote, local):
-        for number, (of_level, of_core, half, place) in enumerate(SOLVERS):
-            if of_level != level:
-                continue
-            src = y_ref.at[level, pl.ds(2 * half, 6)]
-
-            def to(slot, target):
-                return send(src, z_ref.at[slot], z_send.at[number], z_recv.at[slot], (leaf, target))
-
-            @pl.when(jnp.logical_and(core == of_core, grp != place))
+    def own_slice(task, act, local=True):
+        root = ROOTS[0][task] + core * (ROOTS[1][task] - ROOTS[0][task])
+        first, slot = lookup(FIRST[task], core, grp), lookup(SLOT[task], core, grp)
+        src = y_ref.at[task]
+
+        @pl.when(jnp.logical_and(first == root, grp != root))
+        def _():
+            act(send(src, z_ref.at[grp], y_send.at[task], z_recv.at[grp], (leaf, root)))
+
+        @pl.when(first != root)
+        def _():
+            act(send(src, relay_ref.at[task, slot], y_send.at[task], relay_recv.at[task, slot], (leaf, first)))
+
+        if local:
+
+            @pl.when(grp == root)
             def _():
-                remote(to(grp, place))
-
-            @pl.when(jnp.logical_and(core == of_core, grp == place))
+                act(pltpu.make_async_copy(src, z_ref.at[grp], z_local))
+
+    def to_root(task):
+        own_slice(task, lambda copy: copy.start())
+
+    def pass_on(task, act):
+        root = ROOTS[0][task] + core * (ROOTS[1][task] - ROOTS[0][task])
+        for slot in range(3):
+            source_grp = lookup(PASS_ON[task][slot], core, grp)
+
+            @pl.when(source_grp > 0)
             def _():
-                local(pltpu.make_async_copy(src, z_ref.at[grp], z_local), to, place)
-
-    def to_solver(level):
-        each_solver(level, lambda copy: copy.start(), lambda copy, to, place: copy.start())
-
-    def solver_end(level):
-        def collect(copy, to, place):
-            copy.wait()
-            for source_grp in range(16):
-                if source_grp != place:
-                    to(source_grp, source_grp).wait_recv()
-
-        each_solver(level, lambda copy: copy.wait_send(), collect)
+                held = relay_ref.at[task, slot]
+                act(
+                    send(held, held, y_send.at[task], relay_recv.at[task, slot], (leaf, root)),
+                    send(held, z_ref.at[source_grp - 1], relay_send.at[task, slot], z_recv.at[source_grp - 1], (leaf, root)),
+                )
+
+    def relay(task):
+        def act(landed, onward):
+            landed.wait_recv()
+            onward.start()
+
+        pass_on(task, act)
 
     def both(first, second):
         return jnp.concatenate([first, second], axis=1)
 
+    to_root(0)
     up = send(y_ref.at[0, pl.ds(2, 4)], r1_ref, leaf_send.at[0], leaf_recv.at[0], (base, grp))
 
     @pl.when(core == 1)
@@ -294,7 +354,6 @@
     part3 = placed[:32] + pltpu.roll(placed[32:], 64, 1)
     a3_ref[...] = part3
     share(7, a3_ref, r4_ref, leaf, 13, 1, (8, 10, 6, 12, 14, 4, 2, 0), part3)
-    to_solver(0)
 
     def arrived(ref, recv, slot):
         @pl.when(slot != lax.rem(leaf, ref.shape[0]))
@@ -309,15 +368,14 @@
         for i in range(2):
             select(1, 2 + i, both(r1_ref[2 * i], r1_ref[2 * i + 1]))
 
-    to_solver(1)
-
     @pl.when(core == 1)
     def _():
         for s in range(4):
             arrived(r2_ref, 1, s)
             select(2, s, both(r2_ref[s, 0], r2_ref[s, 1]))
 
-    to_solver(2)
+    to_root(1)
+    relay(0)
 
     @pl.when(core == 0)
     def _():
@@ -325,8 +383,6 @@
             arrived(r3_ref, 5, 2 * s)
             arrived(r3_ref, 5, 2 * s + 1)
             select(3, s, both(r3_ref[2 * s], r3_ref[2 * s + 1]))
-
-    to_solver(3)
 
     @pl.when(core == 1)
     def _():
@@ -342,22 +398,160 @@
         for s in range(4):
             select(4, s, both(joined[2 * s], joined[2 * s + 1]))
 
-    to_solver(4)
-
-    top = send(y_ref.at[4, pl.ds(2, 4)], y_ref.at[4, pl.ds(2, 4)], leaf_send.at[15], leaf_recv.at[29], (base, grp))
+    to_root(2)
+    relay(1)
+    relay(2)
+
+    top = send(y_ref.at[2, pl.ds(2, 4)], rt_ref, leaf_send.at[15], leaf_recv.at[29], (base, grp))
 
     @pl.when(core == 1)
     def _():
         top.start()
+
+    earlier = jnp.where(
+        lax.broadcasted_iota(jnp.int32, (64, 64), 1) < lax.broadcasted_iota(jnp.int32, (64, 64), 0), 1.0, 0.0
+    ).astype(jnp.bfloat16)
+    ones = jnp.full((512, 128), 1.0, jnp.bfloat16)
+    for level in range(5):
+        node = 32 - (32 >> level) + leaf // (1 << level)
+        place = grp * 64 + lax.broadcasted_iota(jnp.int32, (64, 512), 0)
+        is_pivot = jnp.where(place == row_of(pivot_ref[...], node), 1.0, 0.0)
+        out_ref[level] = is_pivot
+        free = 1.0 - jnp.dot(is_pivot.astype(jnp.bfloat16), ones, preferred_element_type=jnp.float32)
+        rank = jnp.dot(earlier, free.astype(jnp.bfloat16), preferred_element_type=jnp.float32)
+        lane = lax.broadcasted_iota(jnp.int32, (64, 128), 1).astype(jnp.float32)
+        spot_ref[level] = jnp.where(jnp.logical_and(free > 0.5, rank == lane), 1.0, 0.0)
+
+    is_main, is_twin = roles()
+    twin_leaf = base + 1 - core
+    coming = ((0, 0), (0, 1), (0, 3), (1, 0), (3, 0), (0, 2), (2, 0), (1, 1), (1, 3), (3, 1), (3, 3), (1, 2), (3, 2), (2, 1), (2, 3), (2, 2))
+
+    def to_twin(at):
+        part = z_ref.at[at, pl.ds(2, 6)]
+        return send(part, part, twin_send.at[at], twin_recv.at[at], (twin_leaf, grp))
+
+    for group in range(4):
+        places = [lax.rem(y + dy, 4) * 4 + lax.rem(x + dx, 4) for dy, dx in coming[4 * group : 4 * group + 4]]
+
+        @pl.when(is_main > 0)
+        def _():
+            for n, at in enumerate(places):
+                if group == 0 and n == 0:
+                    pltpu.make_async_copy(y_ref.at[0], z_ref.at[at], z_local).wait()
+                else:
+                    send(y_ref.at[0], z_ref.at[at], y_send.at[0], z_recv.at[at], (twin_leaf, grp)).wait_recv()
+                to_twin(at).start()
+
+        @pl.when(is_twin > 0)
+        def _():
+            for at in places:
+                to_twin(at).wait_recv()
+
+        @pl.when(is_main + is_twin > 0)
+        def _():
+            rows = []
+            for at in places:
+                blocks = [z_ref[at, 2 + b] for b in range(4)] + [z_ref[at, 6 * is_twin + b] for b in range(2)]
+                rows.append(jnp.concatenate(blocks, axis=1))
+            z = jnp.concatenate(rows, axis=0)
+            gram = lax.dot_general(
+                z, z[:, :512], (((0,), (0,)), ((), ())), precision=HI, preferred_element_type=jnp.float32
+            )
+            if group == 0:
+                m_ref[...] = gram
+            else:
+                m_ref[...] += gram
+
+    @pl.when(is_main + is_twin > 0)
+    def _():
+        solve_in_place(m_ref)
+
+    def each(level, of_core, half, place, to_core, act):
+        @pl.when(jnp.logical_and(core == of_core, grp == place))
+        def _():
+            for target in range(8 * half, 8 * half + 8):
+                if (target, to_core) != (place, of_core):
+                    act(
+                        send(
+                            m_ref.at[pl.ds(512 + 32 * (target - 8 * half), 32)], rows_ref.at[level],
+                            u_send.at[target], u_recv.at[level], (base + to_core, target),
+                        )
+                    )
+
+    for sender in senders():
+        each(*sender, lambda copy: copy.start())
+
+    block_half = grp // 8
+
+    def onward(level):
+        return send(rows_ref.at[level], rows_ref.at[level], u_onward.at[level], u_recv.at[level], (twin_leaf, grp))
+
+    def served_here(of_core):
+        return core == of_core + block_half * (1 - 2 * of_core)
+
+    for of_core in range(2):
+        for task in range(3):
+            level, root = LEVELS[of_core][task], ROOTS[of_core][task]
+            direct = core == of_core if task == 0 else served_here(of_core)
+            is_root = grp == root
+            if task == 0:
+                is_root = jnp.logical_and(is_root, block_half == 0)
+
+            @pl.when(jnp.logical_and(direct, is_root))
+            def _():
+                low = 512 + 32 * (root % 8)
+                rows_ref[level] = m_ref[low : low + 32, :]
+
+            @pl.when(jnp.logical_and(direct, jnp.logical_not(is_root)))
+            def _():
+                onward(level).wait_recv()
+
+            if task > 0:
+
+                @pl.when(direct)
+                def _():
+                    onward(level).start()
+
+    for of_core in range(2):
+        for task in (1, 2):
+            level = LEVELS[of_core][task]
+
+            @pl.when(jnp.logical_not(served_here(of_core)))
+            def _():
+                onward(level).wait_recv()
+
+    for level in range(5):
+        out_ref[level] += lax.dot_general(
+            spot_ref[level][:, :32], rows_ref[level], (((1,), (0,)), ((), ())),
+            precision=HI, preferred_element_type=jnp.float32,
+        )
+    for sender in senders():
+        each(*sender, lambda copy: copy.wait_send())
+    for of_core in range(2):
+        for task in (1, 2):
+            level = LEVELS[of_core][task]
+
+            @pl.when(served_here(of_core))
+            def _():
+                onward(level).wait_send()
+
+    @pl.when(core == 1)
+    def _():
+        for b in range(4):
+            top_ref[:, 128 * b : 128 * b + 128] = y_ref[2, 2 + b]
         up.wait_send()
         top.wait_send()
 
     @pl.when(core == 0)
     def _():
         top.wait_recv()
-
-    for b in range(4):
-        top_ref[:, 128 * b : 128 * b + 128] = y_ref[4, 2 + b]
+        for b in range(4):
+            top_ref[:, 128 * b : 128 * b + 128] = rt_ref[b]
+
+    @pl.when(is_main > 0)
+    def _():
+        for at in range(16):
+            to_twin(at).wait_send()
 
     for copy, to_core in kept:
 
@@ -367,8 +561,9 @@
 
     for copy in started:
         copy.wait_send()
-    for level in range(5):
-        solver_end(level)
+    for task in range(3):
+        own_slice(task, lambda copy: copy.wait_send(), local=False)
+        pass_on(task, lambda landed, onward: onward.wait_send())
 
 
 def gathered(front_rows, sample_matrix, pivots):
@@ -379,113 +574,31 @@
     vmem = pl.BlockSpec(memory_space=pltpu.VMEM)
     return pl.pallas_call(
         gather_kernel,
-        out_shape=(jax.ShapeDtypeStruct((16, 6, 64, 128), jnp.float32), jax.ShapeDtypeStruct((64, 512), jnp.float32)),
+        out_shape=(jax.ShapeDtypeStruct((5, 64, 512), jnp.float32), jax.ShapeDtypeStruct((64, 512), jnp.float32)),
         in_specs=[anywhere, anywhere, vmem],
-        out_specs=(anywhere, vmem),
+        out_specs=(vmem, vmem),
         scratch_shapes=[
             bf16(1024, 1536), bf16(1536, 1024), bf16(1024, 1536), f32(4, 4, 64, 1024),
             f32(4, 2, 2, 64, 256), f32(4, 2, 2, 64, 256), f32(4, 2, 4, 64, 256), f32(4, 4, 64, 256),
-            f32(4, 2, 32, 256), f32(4, 2, 32, 256), f32(4, 2, 64, 256), bf16(20, 256, 256), f32(5, 8, 64, 128),
+            f32(4, 2, 32, 256), f32(4, 2, 32, 256), f32(4, 2, 64, 256), bf16(20, 256, 256), f32(3, 8, 64, 128),
             f32(2, 64, 128), f32(64, 128), f32(32, 128), f32(4, 64, 128), f32(4, 2, 64, 128), f32(8, 64, 128), f32(16, 32, 128),
-            dma((2,)), dma((2, 4, 2, 3)), dma((2, 4, 2, 3)), dma((16,)), dma((30,)), dma((12,)), dma((16,)), dma,
+            f32(4, 64, 128), f32(3, 3, 8, 64, 128), f32(16, 8, 64, 128),
+            f32(768, 512), f32(5, 64, 128), f32(5, 32, 512),
+            dma((2,)), dma((2, 4, 2, 3)), dma((2, 4, 2, 3)), dma((16,)), dma((30,)),
+            dma((3,)), dma((3, 3)), dma((3, 3)), dma((16,)), dma, dma((16,)), dma((16,)),
+            dma((16,)), dma((5,)), dma((5,)),
         ],
         compiler_params=pltpu.CompilerParams(collective_id=1, has_side_effects=True, vmem_limit_bytes=56 * 1024 * 1024),
     )(front_rows, sample_matrix, pivots)
 
 
-def solver_role():
-    grp, core = lax.axis_index("grp"), lax.rem(lax.axis_index("leaf"), 2)
-    active, half = 0, 0
-    for _, of_core, of_half, place in SOLVERS:
-        here = jnp.where(jnp.logical_and(core == of_core, grp == place), 1, 0)
-        active, half = active + here, half + of_half * here
-    return active > 0, half
-
-
-def spread_kernel(u_ref, pivot_ref, out_ref, rows_ref, u_send, u_recv, u_local):
-    leaf, grp = lax.axis_index("leaf"), lax.axis_index("grp")
-    core = lax.rem(leaf, 2)
-    base = leaf - core
-    barrier = pltpu.get_barrier_semaphore()
-    for other in range(1, 16):
-        pl.semaphore_signal(barrier, inc=1, device_id=(leaf, lax.rem(grp + other, 16)), device_id_type=MESH)
-    for other in range(16):
-        pl.semaphore_signal(barrier, inc=1, device_id=(base + 1 - core, other), device_id_type=MESH)
-    pl.semaphore_wait(barrier, 31)
-
-    def each(level, of_core, half, place, act):
-        def to(target_core, target, slot):
-            return send(
-                u_ref.at[pl.ds(32 * (target - 8 * half), 32)], rows_ref.at[level], u_send.at[slot], u_recv.at[level],
-                (base + target_core, target),
-            )
-
-        @pl.when(jnp.logical_and(core == of_core, grp == place))
-        def _():
-            for target in range(8 * half, 8 * half + 8):
-                if target != place:
-                    act(to(of_core, target, target))
-                if level > 0:
-                    act(to(1 - of_core, target, 16 + target))
-
-    for solver in SOLVERS:
-        each(*solver, lambda copy: copy.start())
-
-    before = jnp.where(
-        lax.broadcasted_iota(jnp.int32, (64, 64), 1) < lax.broadcasted_iota(jnp.int32, (64, 64), 0), 1.0, 0.0
-    ).astype(jnp.bfloat16)
-    ones = jnp.full((512, 128), 1.0, jnp.bfloat16)
-    spots = []
-    for level in range(5):
-        node = 32 - (32 >> level) + leaf // (1 << level)
-        at = grp * 64 + lax.broadcasted_iota(jnp.int32, (64, 512), 0)
-        is_pivot = jnp.where(at == row_of(pivot_ref[...], node), 1.0, 0.0)
-        out_ref[level] = is_pivot
-        free = 1.0 - jnp.dot(is_pivot.astype(jnp.bfloat16), ones, preferred_element_type=jnp.float32)
-        rank = jnp.dot(before, free.astype(jnp.bfloat16), preferred_element_type=jnp.float32)
-        slot = lax.broadcasted_iota(jnp.int32, (64, 128), 1).astype(jnp.float32)
-        spots.append(jnp.where(jnp.logical_and(free > 0.5, rank == slot), 1.0, 0.0)[:, :32])
-
-    for level, of_core, half, place in SOLVERS:
-        own = jnp.logical_and(core == of_core, grp == place)
-        if place // 8 == half:
-
-            @pl.when(own)
-            def _():
-                copy = pltpu.make_async_copy(u_ref.at[pl.ds(32 * (place - 8 * half), 32)], rows_ref.at[level], u_local)
-                copy.start()
-                copy.wait()
-
-            gets = jnp.logical_and(grp // 8 == half, jnp.logical_not(own))
-        else:
-            gets = grp // 8 == half
-        if level == 0:
-            gets = jnp.logical_and(core == of_core, gets)
-
-        @pl.when(gets)
-        def _():
-            send(
-                u_ref.at[pl.ds(0, 32)], rows_ref.at[level], u_send.at[0], u_recv.at[level], (base + 1 - core, grp)
-            ).wait_recv()
-
-    for level in range(5):
-        out_ref[level] += lax.dot_general(
-            spots[level], rows_ref[level], (((1,), (0,)), ((), ())), precision=HI, preferred_element_type=jnp.float32
-        )
-    for solver in SOLVERS:
-        each(*solver, lambda copy: copy.wait_send())
-
-
-def spread(u, pivots):
-    dma = pltpu.SemaphoreType.DMA
-    return pl.pallas_call(
-        spread_kernel,
-        out_shape=jax.ShapeDtypeStruct((5, 64, 512), jnp.float32),
-        in_specs=[pl.BlockSpec(memory_space=pltpu.VMEM)] * 2,
-        out_specs=pl.BlockSpec(memory_space=pltpu.VMEM),
-        scratch_shapes=[pltpu.VMEM((5, 32, 512), jnp.float32), dma((32,)), dma((5,)), dma],
-        compiler_params=pltpu.CompilerParams(collective_id=2, has_side_effects=True, vmem_limit_bytes=16 * 1024 * 1024),
-    )(u, pivots)
+def senders():
+    for core in range(2):
+        for task in range(3):
+            level, root = LEVELS[core][task], ROOTS[core][task]
+            for half in range(2):
+                sender = core if half == 0 else 1 - core
+                yield level, sender, half, root, core if level == 0 else sender
 
 
 def wide(value):
@@ -538,55 +651,21 @@
     return lax.dot_general(a, b, (((1,), (0,)), ((), ())), precision=HI, preferred_element_type=jnp.float32)
 
 
-def solve_kernel(z_ref, u_ref, m_ref):
-    step = pl.program_id(0)
-    active, half = solver_role()
-
-    @pl.when(step == 0)
-    def _():
-        m_ref[...] = jnp.zeros_like(m_ref)
-
-    @pl.when(active)
-    def _():
-        rows = []
-        for g in range(4):
-            skeleton = [z_ref[g, 2 - 2 * half + b] for b in range(4)]
-            rows.append(jnp.concatenate(skeleton + [z_ref[g, 4 * half + b] for b in range(2)], axis=1))
-        z = jnp.concatenate(rows, axis=0)
-        m_ref[...] += lax.dot_general(
-            z, z[:, :512], (((0,), (0,)), ((), ())), precision=HI, preferred_element_type=jnp.float32
-        )
-
-    @pl.when(jnp.logical_and(active, step == 3))
-    def _():
-        for p in range(4):
-            at = 128 * p
-            dinv = invert(lambda i: m_ref[at + 8 * i : at + 8 * i + 8, at : at + 128])
-            lead = m_ref[at : at + 128, :]
-            for low in range(at + 128, 768, 128):
-                w = dot(m_ref[low : low + 128, at : at + 128], dinv)
-                for q in range(4):
-                    if q != p:
-                        m_ref[low : low + 128, 128 * q : 128 * q + 128] -= dot(w, lead[:, 128 * q : 128 * q + 128])
-                m_ref[low : low + 128, at : at + 128] = w
-        u_ref[...] = m_ref[512:, :]
-
-
-def solve(z):
-    return pl.pallas_call(
-        solve_kernel,
-        grid=(4,),
-        in_specs=[pl.BlockSpec((4, 6, 64, 128), lambda i: (i, 0, 0, 0))],
-        out_specs=pl.BlockSpec((256, 512), lambda i: (0, 0)),
-        out_shape=jax.ShapeDtypeStruct((256, 512), jnp.float32),
-        scratch_shapes=[pltpu.VMEM((768, 512), jnp.float32)],
-        compiler_params=pltpu.CompilerParams(dimension_semantics=("arbitrary",), vmem_limit_bytes=56 * 1024 * 1024),
-    )(z)
+def solve_in_place(m_ref):
+    for p in range(4):
+        at = 128 * p
+        dinv = invert(lambda i: m_ref[at + 8 * i : at + 8 * i + 8, at : at + 128])
+        lead = m_ref[at : at + 128, :]
+        for low in range(at + 128, 768, 128):
+            w = dot(m_ref[low : low + 128, at : at + 128], dinv)
+            for q in range(4):
+                if q != p:
+                    m_ref[low : low + 128, 128 * q : 128 * q + 128] -= dot(w, lead[:, 128 * q : 128 * q + 128])
+            m_ref[low : low + 128, at : at + 128] = w
 
 
 def on_device(front_rows, sample_matrix, pivots):
-    z, top = gathered(front_rows, sample_matrix, pivots)
-    bases = spread(solve(z), pivots)
+    bases, top = gathered(front_rows, sample_matrix, pivots)
     return (bases[:, None], top)
 
 

time: 119 us -> 113 us (0.950)
  the two profiles are of different devices: /device:TPU:8 before, /device:TPU:30 now
where the time goes in v4:
time: 113 us; the launch traced here: 112 us
  Pallas kernels  108 us (96%)
  local copies, waits for them, and re-layouts  3.56 us (3%)
    pallas_call x1, Pallas kernels, gathered(): pl.pallas_call(gather_kernel, out_shape=(jax.ShapeDtypeStruct((5, 64, 512...  108 us
    unnamed x2, local copies, waits for them, and re-layouts  3.56 us

profile of v4, /device:TPU:30, one launch (start us, length us, event | category | flops | bytes accessed | tf_op | source)
XLA Modules:
  0.0 112.3 jit_solution(9675319391255752053)
XLA Ops:
  0.6 108.1 %shard_map.50 = (f32[5,64,512]{2,1,0:T(8,128)}, f32[64,512]{1,0:T(8,128)}) custom-call(bf16[1024,1536]{1,0:T(8,128)(2,1)} %front_any.1, bf16[1536,1024]{1,0:T(8,128)(2,1)} %sample_any.1, s32[31,512]{1,0:T(8,128)} %pivot_ref.1), custom_call_target="tpu_custom_call" | custom-call | tf_op jit(solution)/shard_map/pallas_call | solution.py:575
  108.8 2.0 %copy.8 = f32[5,1,64,512]{3,2,1,0:T(8,128)} copy(f32[5,1,64,512]{3,2,1,0:T(8,128)} %bitcast.3) | data formatting | bytes 1310720
  110.8 1.6 %copy.9 = f32[64,512]{1,0:T(8,128)} copy(f32[64,512]{1,0:T(8,128)} %get-tuple-element.11) | data formatting | bytes 262144

commit v5 on v4

--- a/solution.py
+++ b/solution.py
@@ -7,6 +7,7 @@
 
 HI = lax.Precision.HIGHEST
 MESH = pl.DeviceIdType.MESH
+PARTS = 2
 ROOTS = ((8, 7, 5), (2, 10, 13))
 LEVELS = ((0, 1, 3), (0, 2, 4))
 FIRST = (
@@ -122,9 +123,12 @@
     base = leaf - core
 
     loads = [
-        pltpu.make_async_copy(sample_any, sample_ref, load_sem.at[0]),
-        pltpu.make_async_copy(front_any, front_ref, load_sem.at[1]),
+        pltpu.make_async_copy(sample_any.at[pl.ds(512 * r, 512)], sample_ref.at[pl.ds(512 * r, 512)], load_sem.at[r])
+        for r in range(3)
     ]
+    for quarter in range(4):
+        rows = pl.ds(512 * (quarter % 2) + 256 * (quarter // 2), 256)
+        loads.append(pltpu.make_async_copy(front_any.at[rows], front_ref.at[rows], load_sem.at[3 + quarter]))
     for load in loads:
         load.start()
     barrier = pltpu.get_barrier_semaphore()
@@ -203,12 +207,15 @@
         own = sum1[stream, position(1, stream)]
         return (near2[stream, 0] + own) + near2[stream, 1]
 
-    loads[0].wait()
-    for c in range(8):
-        turned_ref[128 * c : 128 * c + 128, :] = sample_ref[:, 128 * c : 128 * c + 128].T
-    loads[1].wait()
-    for stream in range(4):
-        low = 512 * (stream % 2) + 256 * (stream // 2)
+    for r in range(3):
+        loads[r].wait()
+        for c in range(8):
+            turned_ref[128 * c : 128 * c + 128, 512 * r : 512 * r + 512] = sample_ref[
+                512 * r : 512 * r + 512, 128 * c : 128 * c + 128
+            ].T
+    for quarter in range(4):
+        low = 512 * (quarter % 2) + 256 * (quarter // 2)
+        loads[3 + quarter].wait()
         for c in range(4):
             product = lax.dot_general(
                 turned_ref[256 * c : 256 * c + 256, :], front_ref[low : low + 256, :], (((1,), (1,)), ((), ())),
@@ -216,11 +223,13 @@
             )
             for b in range(4):
                 p_ref[c, b, :, low : low + 256] = product[64 * b : 64 * b + 64]
-        if stream == 0:
+        if quarter == 0:
             pl.semaphore_wait(barrier, 30)
-        ring_hop(0, stream)
-        if stream < 2:
-            ring_own(0, stream)
+        for n in range(PARTS // 2):
+            stream = quarter % 2 + 2 * (PARTS // 2 * (quarter // 2) + n)
+            ring_hop(0, stream)
+            if stream < 2:
+                ring_own(0, stream)
 
     def orders(level, block):
         node = 32 - (32 >> level) + leaf // (1 << level)
@@ -228,42 +237,41 @@
         order_ref[4 * level + block, :, 0:128] = chosen
         order_ref[4 * level + block, :, 128:256] = rest
 
-    for block in range(4):
-        orders(0, block)
-        orders(1, block)
-    ring_join(0, 0)
-    ring_join(0, 1)
-    ring_own(0, 2)
-    ring_own(0, 3)
-    for block in range(4):
-        orders(2, block)
-        orders(3, block)
-        orders(4, block)
-    for stream in (0, 1):
-        ring_last(0, stream)
-        ring_hop(1, stream)
-        ring_own(1, stream)
-    ring_join(0, 2)
-    ring_join(0, 3)
-    ring_join(1, 0)
-    ring_join(1, 1)
-    for stream in (2, 3):
-        ring_last(0, stream)
-        ring_hop(1, stream)
-        ring_own(1, stream)
-
     def select(level, block, value):
         chosen = permuted(value, order_ref[4 * level + block])
         task = (level + 1) // 2
         y_ref[task, 2 + block] = chosen[:, :128]
         y_ref[task, block + 4 * (block // 2)] = chosen[:, 128:]
 
-    select(0, 0, ring_last(1, 0))
-    select(0, 2, ring_last(1, 1))
-    ring_join(1, 2)
-    ring_join(1, 3)
-    select(0, 1, ring_last(1, 2))
-    select(0, 3, ring_last(1, 3))
+    done = {}
+    for step in range(PARTS + 3):
+        if step < PARTS:
+            for half in range(2):
+                ring_join(0, 2 * step + half)
+            if step + 1 < PARTS:
+                for half in range(2):
+                    ring_own(0, 2 * step + 2 + half)
+        if step == 0:
+            for level in range(5):
+                for block in range(4):
+                    orders(level, block)
+        if 1 <= step <= PARTS:
+            for half in range(2):
+                ring_last(0, 2 * step - 2 + half)
+                ring_hop(1, 2 * step - 2 + half)
+                ring_own(1, 2 * step - 2 + half)
+        if 2 <= step <= PARTS + 1:
+            for half in range(2):
+                ring_join(1, 2 * step - 4 + half)
+        if step >= 3:
+            part = step - 3
+            for half in range(2):
+                done[half, part] = ring_last(1, 2 * part + half)
+            each = PARTS // 2
+            if (part + 1) % each == 0:
+                for half in range(2):
+                    value = jnp.concatenate([done[half, part + 1 - each + n] for n in range(each)], axis=1)
+                    select(0, 2 * half + part // each, value)
 
     def own_slice(task, act, local=True):
         root = ROOTS[0][task] + core * (ROOTS[1][task] - ROOTS[0][task])
@@ -521,9 +529,9 @@
                 onward(level).wait_recv()
 
     for level in range(5):
-        out_ref[level] += lax.dot_general(
-            spot_ref[level][:, :32], rows_ref[level], (((1,), (0,)), ((), ())),
-            precision=HI, preferred_element_type=jnp.float32,
+        spot = spot_ref[level][:, :32].astype(jnp.bfloat16)
+        out_ref[level] += jnp.dot(
+            jnp.concatenate([spot, spot, spot], axis=1), split3(rows_ref[level]), preferred_element_type=jnp.float32
         )
     for sender in senders():
         each(*sender, lambda copy: copy.wait_send())
@@ -584,11 +592,11 @@
             f32(2, 64, 128), f32(64, 128), f32(32, 128), f32(4, 64, 128), f32(4, 2, 64, 128), f32(8, 64, 128), f32(16, 32, 128),
             f32(4, 64, 128), f32(3, 3, 8, 64, 128), f32(16, 8, 64, 128),
             f32(768, 512), f32(5, 64, 128), f32(5, 32, 512),
-            dma((2,)), dma((2, 4, 2, 3)), dma((2, 4, 2, 3)), dma((16,)), dma((30,)),
+            dma((7,)), dma((2, 4, 2, 3)), dma((2, 4, 2, 3)), dma((16,)), dma((30,)),
             dma((3,)), dma((3, 3)), dma((3, 3)), dma((16,)), dma, dma((16,)), dma((16,)),
             dma((16,)), dma((5,)), dma((5,)),
         ],
-        compiler_params=pltpu.CompilerParams(collective_id=1, has_side_effects=True, vmem_limit_bytes=56 * 1024 * 1024),
+        compiler_params=pltpu.CompilerParams(collective_id=1, has_side_effects=True, vmem_limit_bytes=44 * 1024 * 1024),
     )(front_rows, sample_matrix, pivots)
 
 
@@ -628,7 +636,7 @@
     return even + odd
 
 
-def invert(read):
+def eliminate(read):
     lane = lax.broadcasted_iota(jnp.int32, (8, 128), 1)
     sub = lax.broadcasted_iota(jnp.int32, (8, 128), 0)
     eye = jnp.where(lane == sub, 1.0, 0.0)
@@ -643,25 +651,47 @@
         rest = [jnp.where(lane < 8, 0.0, block) - weighted(cols, rows) for cols, block in zip(columns, rolled[1:])]
         return tuple(rest + [new])
 
-    blocks = lax.fori_loop(0, 16, eight, tuple(pltpu.roll(read(i), 8, 1) for i in range(16)))
-    return jnp.concatenate([pltpu.roll(block, 120, 1) for block in blocks], axis=0)
+    blocks = lax.fori_loop(0, 8, eight, tuple(pltpu.roll(read(i), 8, 1) for i in range(8)))
+    return jnp.concatenate([pltpu.roll(block, 56, 1) for block in blocks], axis=0)
+
+
+def invert(block):
+    upper, lower = block[:64], block[64:]
+    lane = lax.broadcasted_iota(jnp.int32, (64, 128), 1)
+    first = eliminate(lambda i: upper[8 * i : 8 * i + 8])
+    reduced = pltpu.roll(jnp.where(lane < 64, 0.0, lower) - dot(lower[:, :64], first), 64, 1)
+    second = eliminate(lambda i: reduced[8 * i : 8 * i + 8])
+    bottom = pltpu.roll(second, 64, 1)
+    across = pltpu.roll(first, 64, 1)[:, :64]
+    top = jnp.where(lane < 64, first, 0.0) - dot(across, bottom)
+    return jnp.concatenate([top, bottom], axis=0)
 
 
 def dot(a, b):
     return lax.dot_general(a, b, (((1,), (0,)), ((), ())), precision=HI, preferred_element_type=jnp.float32)
+
+
+def dot6(a, b):
+    n = a.shape[0]
+    ah, am, al = (split3(a)[k * n : k * n + n] for k in range(3))
+    bh, bm, bl = (split3(b)[k * 128 : k * 128 + 128] for k in range(3))
+    left1 = jnp.concatenate([ah, am], axis=1)
+    d = lambda u, v: jnp.dot(u, v, preferred_element_type=jnp.float32)
+    small = d(left1, jnp.concatenate([bl, bm], axis=0)) + d(jnp.concatenate([al, am], axis=1), jnp.concatenate([bh, bh], axis=0))
+    return small + d(jnp.concatenate([ah, ah], axis=1), jnp.concatenate([bm, bh], axis=0))
 
 
 def solve_in_place(m_ref):
     for p in range(4):
         at = 128 * p
-        dinv = invert(lambda i: m_ref[at + 8 * i : at + 8 * i + 8, at : at + 128])
-        lead = m_ref[at : at + 128, :]
-        for low in range(at + 128, 768, 128):
-            w = dot(m_ref[low : low + 128, at : at + 128], dinv)
-            for q in range(4):
-                if q != p:
-                    m_ref[low : low + 128, 128 * q : 128 * q + 128] -= dot(w, lead[:, 128 * q : 128 * q + 128])
-            m_ref[low : low + 128, at : at + 128] = w
+        dinv = invert(m_ref[at : at + 128, at : at + 128])
+        others = [q for q in range(4) if q != p]
+        lead = jnp.concatenate([m_ref[at : at + 128, 128 * q : 128 * q + 128] for q in others], axis=1)
+        both_sides = dot(dinv, lead)
+        change = dot6(m_ref[at + 128 :, at : at + 128], jnp.concatenate([both_sides, dinv], axis=1))
+        for n, q in enumerate(others):
+            m_ref[at + 128 :, 128 * q : 128 * q + 128] -= change[:, 128 * n : 128 * n + 128]
+        m_ref[at + 128 :, at : at + 128] = change[:, 384:]
 
 
 def on_device(front_rows, sample_matrix, pivots):

time: 113 us -> 106 us (0.938)
  Pallas kernels: 108 us -> 99.1 us
  local copies, waits for them, and re-layouts: 3.56 us -> 6.1 us
    pallas_call x1, Pallas kernels: 108 us -> 99.1 us  [gathered(): pl.pallas_call(gather_kernel, out_shape=(jax.ShapeDtypeStruct((5, 64, 512...]
    unnamed x2 -> x8, local copies, waits for them, and re-layouts: 3.56 us -> 6.1 us
where the time goes in v5:
time: 106 us
  Pallas kernels  99.1 us (93%)
  local copies, waits for them, and re-layouts  6.1 us (6%)
    pallas_call x1, Pallas kernels, gathered(): pl.pallas_call(gather_kernel, out_shape=(jax.ShapeDtypeStruct((5, 64, 512...  99.1 us
    unnamed x8, local copies, waits for them, and re-layouts  6.1 us

profile of v5, /device:TPU:30, one launch (start us, length us, event | category | flops | bytes accessed | tf_op | source)
XLA Modules:
  0.0 105.8 jit_solution(14979617165698919355)
XLA Ops:
  0.6 0.0 copy-start
  0.6 1.9 %copy-done = bf16[1024,1536]{1,0:T(8,128)(2,1)S(1)} copy-done((bf16[1024,1536]{1,0:T(8,128)(2,1)S(1)}, bf16[1024,1536]{1,0:T(8,128)(2,1)}, u32[]{:S(2)}) %copy-start) | copy-done | bytes 3145752
  2.5 0.0 copy-start.1
  2.5 1.9 %copy-done.1 = bf16[1536,1024]{1,0:T(8,128)(2,1)S(1)} copy-done((bf16[1536,1024]{1,0:T(8,128)(2,1)S(1)}, bf16[1536,1024]{1,0:T(8,128)(2,1)}, u32[]{:S(2)}) %copy-start.1) | copy-done | bytes 3145752
  4.4 0.0 copy-start.2
  4.4 0.8 copy-done.2
  5.3 99.1 %shard_map.50 = (f32[5,64,512]{2,1,0:T(8,128)S(1)}, f32[64,512]{1,0:T(8,128)S(1)}) custom-call(bf16[1024,1536]{1,0:T(8,128)(2,1)S(1)} %copy-done, bf16[1536,1024]{1,0:T(8,128)(2,1)S(1)} %copy-done.1, s32[31,512]{1,0:T(8,128)S(1)} %copy-done.2), custom_call_target="tpu_custom_call" | custom-call | tf_op jit(solution)/shard_map/pallas_call | solution.py:583
  104.3 0.8 copy.8
  105.2 0.7 copy.9
Async XLA Ops:
  0.6 1.9 %copy-start = (bf16[1024,1536]{1,0:T(8,128)(2,1)S(1)}, bf16[1024,1536]{1,0:T(8,128)(2,1)}, u32[]{:S(2)}) copy-start(bf16[1024,1536]{1,0:T(8,128)(2,1)} %front_any.1) | copy-start | bytes 9437188
  2.5 1.9 %copy-start.1 = (bf16[1536,1024]{1,0:T(8,128)(2,1)S(1)}, bf16[1536,1024]{1,0:T(8,128)(2,1)}, u32[]{:S(2)}) copy-start(bf16[1536,1024]{1,0:T(8,128)(2,1)} %sample_any.1) | copy-start | bytes 9437188
  4.4 0.8 copy-start.2

commit v6 on v5

--- a/solution.py
+++ b/solution.py
@@ -596,7 +596,7 @@
             dma((3,)), dma((3, 3)), dma((3, 3)), dma((16,)), dma, dma((16,)), dma((16,)),
             dma((16,)), dma((5,)), dma((5,)),
         ],
-        compiler_params=pltpu.CompilerParams(collective_id=1, has_side_effects=True, vmem_limit_bytes=44 * 1024 * 1024),
+        compiler_params=pltpu.CompilerParams(collective_id=1, has_side_effects=True, vmem_limit_bytes=52 * 1024 * 1024),
     )(front_rows, sample_matrix, pivots)
 
 

time: 106 us -> 102 us (0.962)
  local copies, waits for them, and re-layouts: 6.1 us -> 2.33 us
    unnamed x8 -> x4, local copies, waits for them, and re-layouts: 6.1 us -> 2.33 us
where the time goes in v6:
time: 102 us
  Pallas kernels  98.6 us (97%)
  local copies, waits for them, and re-layouts  2.33 us (2%)
    pallas_call x1, Pallas kernels, gathered(): pl.pallas_call(gather_kernel, out_shape=(jax.ShapeDtypeStruct((5, 64, 512...  98.6 us
    unnamed x4, local copies, waits for them, and re-layouts  2.33 us

profile of v6, /device:TPU:30, one launch (start us, length us, event | category | flops | bytes accessed | tf_op | source)
XLA Modules:
  0.0 101.5 jit_solution(2255268619473285101)
XLA Ops:
  0.6 0.0 copy-start
  0.6 0.8 copy-done
  1.5 98.6 %shard_map.50 = (f32[5,64,512]{2,1,0:T(8,128)S(1)}, f32[64,512]{1,0:T(8,128)S(1)}) custom-call(bf16[1024,1536]{1,0:T(8,128)(2,1)} %front_any.1, bf16[1536,1024]{1,0:T(8,128)(2,1)} %sample_any.1, s32[31,512]{1,0:T(8,128)S(1)} %copy-done), custom_call_target="tpu_custom_call" | custom-call | tf_op jit(solution)/shard_map/pallas_call | solution.py:583
  100.0 0.8 copy.8
  100.9 0.7 copy.9
Async XLA Ops:
  0.6 0.8 copy-start

commit v7 on v6

--- a/solution.py
+++ b/solution.py
@@ -276,21 +276,28 @@
     def own_slice(task, act, local=True):
         root = ROOTS[0][task] + core * (ROOTS[1][task] - ROOTS[0][task])
         first, slot = lookup(FIRST[task], core, grp), lookup(SLOT[task], core, grp)
-        src = y_ref.at[task]
+        pieces = [(part, y_ref.at[task, pl.ds(4 * part, 4)], pl.ds(4 * part, 4)) for part in range(2)]
 
         @pl.when(jnp.logical_and(first == root, grp != root))
         def _():
-            act(send(src, z_ref.at[grp], y_send.at[task], z_recv.at[grp], (leaf, root)))
+            for part, src, blocks in pieces:
+                act(send(src, z_ref.at[grp, blocks], y_send.at[task, part], z_recv.at[grp, part], (leaf, root)))
 
         @pl.when(first != root)
         def _():
-            act(send(src, relay_ref.at[task, slot], y_send.at[task], relay_recv.at[task, slot], (leaf, first)))
+            for part, src, blocks in pieces:
+                act(
+                    send(
+                        src, relay_ref.at[task, slot, blocks],
+                        y_send.at[task, part], relay_recv.at[task, slot, part], (leaf, first),
+                    )
+                )
 
         if local:
 
             @pl.when(grp == root)
             def _():
-                act(pltpu.make_async_copy(src, z_ref.at[grp], z_local))
+                act(pltpu.make_async_copy(y_ref.at[task], z_ref.at[grp], z_local))
 
     def to_root(task):
         own_slice(task, lambda copy: copy.start())
@@ -302,11 +309,16 @@
 
             @pl.when(source_grp > 0)
             def _():
-                held = relay_ref.at[task, slot]
-                act(
-                    send(held, held, y_send.at[task], relay_recv.at[task, slot], (leaf, root)),
-                    send(held, z_ref.at[source_grp - 1], relay_send.at[task, slot], z_recv.at[source_grp - 1], (leaf, root)),
-                )
+                for part in range(2):
+                    blocks = pl.ds(4 * part, 4)
+                    held = relay_ref.at[task, slot, blocks]
+                    act(
+                        send(held, held, y_send.at[task, part], relay_recv.at[task, slot, part], (leaf, root)),
+                        send(
+                            held, z_ref.at[source_grp - 1, blocks],
+                            relay_send.at[task, slot, part], z_recv.at[source_grp - 1, part], (leaf, root),
+                        ),
+                    )
 
     def relay(task):
         def act(landed, onward):
@@ -447,7 +459,9 @@
                 if group == 0 and n == 0:
                     pltpu.make_async_copy(y_ref.at[0], z_ref.at[at], z_local).wait()
                 else:
-                    send(y_ref.at[0], z_ref.at[at], y_send.at[0], z_recv.at[at], (twin_leaf, grp)).wait_recv()
+                    for part in range(2):
+                        piece = z_ref.at[at, pl.ds(4 * part, 4)]
+                        send(piece, piece, y_send.at[0, part], z_recv.at[at, part], (twin_leaf, grp)).wait_recv()
                 to_twin(at).start()
 
         @pl.when(is_twin > 0)
@@ -593,7 +607,7 @@
             f32(4, 64, 128), f32(3, 3, 8, 64, 128), f32(16, 8, 64, 128),
             f32(768, 512), f32(5, 64, 128), f32(5, 32, 512),
             dma((7,)), dma((2, 4, 2, 3)), dma((2, 4, 2, 3)), dma((16,)), dma((30,)),
-            dma((3,)), dma((3, 3)), dma((3, 3)), dma((16,)), dma, dma((16,)), dma((16,)),
+            dma((3, 2)), dma((3, 3, 2)), dma((3, 3, 2)), dma((16, 2)), dma, dma((16,)), dma((16,)),
             dma((16,)), dma((5,)), dma((5,)),
         ],
         compiler_params=pltpu.CompilerParams(collective_id=1, has_side_effects=True, vmem_limit_bytes=52 * 1024 * 1024),
@@ -659,11 +673,11 @@
     upper, lower = block[:64], block[64:]
     lane = lax.broadcasted_iota(jnp.int32, (64, 128), 1)
     first = eliminate(lambda i: upper[8 * i : 8 * i + 8])
-    reduced = pltpu.roll(jnp.where(lane < 64, 0.0, lower) - dot(lower[:, :64], first), 64, 1)
+    reduced = pltpu.roll(jnp.where(lane < 64, 0.0, lower) - product(lower[:, :64], first), 64, 1)
     second = eliminate(lambda i: reduced[8 * i : 8 * i + 8])
     bottom = pltpu.roll(second, 64, 1)
     across = pltpu.roll(first, 64, 1)[:, :64]
-    top = jnp.where(lane < 64, first, 0.0) - dot(across, bottom)
+    top = jnp.where(lane < 64, first, 0.0) - product(across, bottom)
     return jnp.concatenate([top, bottom], axis=0)
 
 
@@ -671,14 +685,13 @@
     return lax.dot_general(a, b, (((1,), (0,)), ((), ())), precision=HI, preferred_element_type=jnp.float32)
 
 
-def dot6(a, b):
-    n = a.shape[0]
+def product(a, b):
+    n, depth = a.shape
     ah, am, al = (split3(a)[k * n : k * n + n] for k in range(3))
-    bh, bm, bl = (split3(b)[k * 128 : k * 128 + 128] for k in range(3))
-    left1 = jnp.concatenate([ah, am], axis=1)
-    d = lambda u, v: jnp.dot(u, v, preferred_element_type=jnp.float32)
-    small = d(left1, jnp.concatenate([bl, bm], axis=0)) + d(jnp.concatenate([al, am], axis=1), jnp.concatenate([bh, bh], axis=0))
-    return small + d(jnp.concatenate([ah, ah], axis=1), jnp.concatenate([bm, bh], axis=0))
+    bh, bm, bl = (split3(b)[k * depth : k * depth + depth] for k in range(3))
+    left = jnp.concatenate([al, am, ah, am, ah, ah], axis=1)
+    right = jnp.concatenate([bh, bm, bl, bh, bm, bh], axis=0)
+    return jnp.dot(left, right, preferred_element_type=jnp.float32)
 
 
 def solve_in_place(m_ref):
@@ -687,8 +700,8 @@
         dinv = invert(m_ref[at : at + 128, at : at + 128])
         others = [q for q in range(4) if q != p]
         lead = jnp.concatenate([m_ref[at : at + 128, 128 * q : 128 * q + 128] for q in others], axis=1)
-        both_sides = dot(dinv, lead)
-        change = dot6(m_ref[at + 128 :, at : at + 128], jnp.concatenate([both_sides, dinv], axis=1))
+        both_sides = product(dinv, lead)
+        change = product(m_ref[at + 128 :, at : at + 128], jnp.concatenate([both_sides, dinv], axis=1))
         for n, q in enumerate(others):
             m_ref[at + 128 :, 128 * q : 128 * q + 128] -= change[:, 128 * n : 128 * n + 128]
         m_ref[at + 128 :, at : at + 128] = change[:, 384:]

time: 102 us -> 100 us (0.980)
  Pallas kernels: 98.6 us -> 97.1 us
    pallas_call x1, Pallas kernels: 98.6 us -> 97.1 us  [gathered(): pl.pallas_call(gather_kernel, out_shape=(jax.ShapeDtypeStruct((5, 64, 512...]
where the time goes in v7:
time: 100 us
  Pallas kernels  97.1 us (97%)
  local copies, waits for them, and re-layouts  2.33 us (2%)
    pallas_call x1, Pallas kernels, gathered(): pl.pallas_call(gather_kernel, out_shape=(jax.ShapeDtypeStruct((5, 64, 512...  97.1 us
    unnamed x4, local copies, waits for them, and re-layouts  2.33 us

profile of v7, /device:TPU:30, one launch (start us, length us, event | category | flops | bytes accessed | tf_op | source)
XLA Modules:
  0.0 100.1 jit_solution(2450195003543934169)
XLA Ops:
  0.6 0.0 copy-start
  0.6 0.8 copy-done
  1.5 97.1 %shard_map.50 = (f32[5,64,512]{2,1,0:T(8,128)S(1)}, f32[64,512]{1,0:T(8,128)S(1)}) custom-call(bf16[1024,1536]{1,0:T(8,128)(2,1)} %front_any.1, bf16[1536,1024]{1,0:T(8,128)(2,1)} %sample_any.1, s32[31,512]{1,0:T(8,128)S(1)} %copy-done), custom_call_target="tpu_custom_call" | custom-call | tf_op jit(solution)/shard_map/pallas_call | solution.py:597
  98.6 0.8 copy.8
  99.4 0.7 copy.9
Async XLA Ops:
  0.6 0.8 copy-start

commit v8 on v7

--- a/solution.py
+++ b/solution.py
@@ -484,14 +484,10 @@
             else:
                 m_ref[...] += gram
 
-    @pl.when(is_main + is_twin > 0)
-    def _():
-        solve_in_place(m_ref)
-
-    def each(level, of_core, half, place, to_core, act):
+    def each(level, of_core, half, place, to_core, act, parts=(0, 1)):
         @pl.when(jnp.logical_and(core == of_core, grp == place))
         def _():
-            for target in range(8 * half, 8 * half + 8):
+            for target in [8 * half + 4 * part + n for part in parts for n in range(4)]:
                 if (target, to_core) != (place, of_core):
                     act(
                         send(
@@ -500,8 +496,13 @@
                         )
                     )
 
-    for sender in senders():
-        each(*sender, lambda copy: copy.start())
+    def rows_ready(part):
+        for sender in senders():
+            each(*sender, lambda copy: copy.start(), (part,))
+
+    @pl.when(is_main + is_twin > 0)
+    def _():
+        solve_in_place(m_ref, rows_ready)
 
     block_half = grp // 8
 
@@ -694,17 +695,22 @@
     return jnp.dot(left, right, preferred_element_type=jnp.float32)
 
 
-def solve_in_place(m_ref):
+def solve_in_place(m_ref, rows_ready):
     for p in range(4):
         at = 128 * p
         dinv = invert(m_ref[at : at + 128, at : at + 128])
         others = [q for q in range(4) if q != p]
         lead = jnp.concatenate([m_ref[at : at + 128, 128 * q : 128 * q + 128] for q in others], axis=1)
         both_sides = product(dinv, lead)
-        change = product(m_ref[at + 128 :, at : at + 128], jnp.concatenate([both_sides, dinv], axis=1))
-        for n, q in enumerate(others):
-            m_ref[at + 128 :, 128 * q : 128 * q + 128] -= change[:, 128 * n : 128 * n + 128]
-        m_ref[at + 128 :, at : at + 128] = change[:, 384:]
+        right = jnp.concatenate([both_sides, dinv], axis=1)
+        bounds = (at + 128, 768) if p < 3 else (512, 640, 768)
+        for part, (low, high) in enumerate(zip(bounds, bounds[1:])):
+            change = product(m_ref[low:high, at : at + 128], right)
+            for n, q in enumerate(others):
+                m_ref[low:high, 128 * q : 128 * q + 128] -= change[:, 128 * n : 128 * n + 128]
+            m_ref[low:high, at : at + 128] = change[:, 384:]
+            if p == 3:
+                rows_ready(part)
 
 
 def on_device(front_rows, sample_matrix, pivots):

time: 100 us -> 100 us (level)
  no operation moved by 1% of the time
where the time goes in v8:
time: 100 us; the launch traced here: 99.8 us
  Pallas kernels  96.9 us (97%)
  local copies, waits for them, and re-layouts  2.33 us (2%)
    pallas_call x1, Pallas kernels, gathered(): pl.pallas_call(gather_kernel, out_shape=(jax.ShapeDtypeStruct((5, 64, 512...  96.9 us
    unnamed x4, local copies, waits for them, and re-layouts  2.33 us

profile of v8, /device:TPU:30, one launch (start us, length us, event | category | flops | bytes accessed | tf_op | source)
XLA Modules:
  0.0 99.8 jit_solution(3474956796433307709)
XLA Ops:
  0.6 0.0 copy-start
  0.6 0.8 copy-done
  1.5 96.9 %shard_map.50 = (f32[5,64,512]{2,1,0:T(8,128)S(1)}, f32[64,512]{1,0:T(8,128)S(1)}) custom-call(bf16[1024,1536]{1,0:T(8,128)(2,1)} %front_any.1, bf16[1536,1024]{1,0:T(8,128)(2,1)} %sample_any.1, s32[31,512]{1,0:T(8,128)S(1)} %copy-done), custom_call_target="tpu_custom_call" | custom-call | tf_op jit(solution)/shard_map/pallas_call | solution.py:598
  98.3 0.8 copy.8
  99.2 0.7 copy.9
Async XLA Ops:
  0.6 0.8 copy-start
